TPU v7x, 32 devices: a 4x4x1 block of a 4x4x8 slice. The times are simulated.
32 devices in a mesh: dp: 1 (over z), ep: 32 (over y, x, core).
Axes of the slice: x: 4, y: 4, z: 1, core: 2. Of those that a mesh axis runs over, the one named last changes fastest.
The devices are a block of a 4x4x8 slice.
Arguments:
- grad_out: bfloat16 [2, 8192, 1024], P(None, ('dp', 'ep'))
- expert_out: bfloat16 [2, 8192, 8, 1024], P(None, ('dp', 'ep'))
- gate_vals: float32 [2, 8192, 8], P(None, ('dp', 'ep'))
- topk_idx: int32 [2, 8192, 8], P(None, ('dp', 'ep'))
- slot_idx: int32 [2, 8192, 8], P(None, ('dp', 'ep'))
- x_dispatch: bfloat16 [2, 32, 2816, 1024], P(None, ('dp', 'ep'))
- h1_pre: bfloat16 [2, 32, 2816, 512], P(None, ('dp', 'ep'))
- h3_pre: bfloat16 [2, 32, 2816, 512], P(None, ('dp', 'ep'))
- w_gate: bfloat16 [32, 1024, 512], P('ep')
- w_up: bfloat16 [32, 1024, 512], P('ep')
- w_down: bfloat16 [32, 512, 1024], P('ep')
Outputs:
- output 1: bfloat16 [2, 8192, 1024], P(None, ('dp', 'ep'))
- output 2: float32 [2, 8192, 8], P(None, ('dp', 'ep'))
- output 3: float32 [32, 1024, 512], P(('dp', 'ep'))
- output 4: float32 [32, 1024, 512], P(('dp', 'ep'))
- output 5: float32 [32, 512, 1024], P(('dp', 'ep'))
All inputs are finite; a program needn't handle non-finite values.
Results may differ from a plain program's by a relative error of at most 0.0116613.
Values are sent between devices in bfloat16 or wider.
A program may use at most 768 MiB of HBM per device.

v0:
```python
import functools
import jax
import jax.numpy as jnp
from jax import lax
from jax.sharding import PartitionSpec as P


def expert_grads(x_rows, h1_rows, h3_rows, dy_rows, w_gate, w_up, w_down):
    h1_f32 = h1_rows.astype(jnp.float32)
    h3_f32 = h3_rows.astype(jnp.float32)
    sigmoid_h1 = jax.nn.sigmoid(h1_f32)
    silu_h1 = h1_f32 * sigmoid_h1
    activation = (silu_h1 * h3_f32).astype(jnp.bfloat16)
    grad_act = jnp.einsum('erd,efd->erf', dy_rows, w_down, preferred_element_type=jnp.float32)
    grad_act = grad_act.astype(jnp.bfloat16).astype(jnp.float32)
    grad_h1 = (grad_act * h3_f32 * sigmoid_h1 * (1.0 + h1_f32 * (1.0 - sigmoid_h1))).astype(jnp.bfloat16)
    grad_h3 = (grad_act * silu_h1).astype(jnp.bfloat16)
    g_down = jnp.einsum('erf,erd->efd', activation, dy_rows, preferred_element_type=jnp.float32)
    g_gate = jnp.einsum('erd,erf->edf', x_rows, grad_h1, preferred_element_type=jnp.float32)
    g_up = jnp.einsum('erd,erf->edf', x_rows, grad_h3, preferred_element_type=jnp.float32)
    dx_rows = jnp.einsum('erf,edf->erd', grad_h1, w_gate, preferred_element_type=jnp.float32)
    dx_rows = (dx_rows + jnp.einsum('erf,edf->erd', grad_h3, w_up, preferred_element_type=jnp.float32)).astype(jnp.bfloat16)
    return g_gate, g_up, g_down, dx_rows


def solution(mesh):
    group_size = mesh.shape['ep']
    tok_spec = P(None, ('dp', 'ep'))
    w_spec = P('ep')
    grad_w_spec = P(('dp', 'ep'))

    def local_step(grad_out, expert_out, gate_vals, topk_idx, slot_idx, x_dispatch, h1_pre, h3_pre, w_gate, w_up, w_down):
        n_micro, tokens, top_k, d_model = expert_out.shape
        local_exp = w_gate.shape[0]
        experts = local_exp * group_size
        capacity = x_dispatch.shape[2] // group_size
        grad_gate = jnp.einsum('mtd,mtkd->mtk', grad_out, expert_out, preferred_element_type=jnp.float32)
        send_rows = jnp.where(slot_idx >= 0, topk_idx * capacity + slot_idx, experts * capacity)
        gated_rows = (gate_vals[:, :, :, None] * grad_out[:, :, None, :].astype(jnp.float32)).astype(jnp.bfloat16)
        dx_list = []
        gate_list = []
        up_list = []
        down_list = []
        for micro_idx in range(n_micro):
            send_buf = jnp.zeros((experts * capacity, d_model), jnp.bfloat16)
            send_buf = send_buf.at[send_rows[micro_idx].reshape(-1)].set(gated_rows[micro_idx].reshape(-1, d_model), mode='drop')
            dy_rows = lax.all_to_all(send_buf.reshape(group_size, local_exp, capacity, d_model), 'ep', 0, 2, tiled=True)
            dy_rows = dy_rows.reshape(local_exp, group_size * capacity, d_model)
            g_gate, g_up, g_down, dx_rows = expert_grads(x_dispatch[micro_idx], h1_pre[micro_idx], h3_pre[micro_idx], dy_rows, w_gate, w_up, w_down)
            returned = lax.all_to_all(dx_rows, 'ep', 1, 0, tiled=True)
            picked = jnp.take(returned.reshape(experts * capacity, d_model), send_rows[micro_idx], axis=0, mode='fill', fill_value=0)
            dx_list.append(jnp.sum(picked, axis=1, dtype=jnp.float32).astype(jnp.bfloat16))
            gate_list.append(g_gate)
            up_list.append(g_up)
            down_list.append(g_down)
        grad_w_gate = functools.reduce(jnp.add, gate_list)
        grad_w_up = functools.reduce(jnp.add, up_list)
        grad_w_down = functools.reduce(jnp.add, down_list)
        return jnp.stack(dx_list), grad_gate, grad_w_gate, grad_w_up, grad_w_down

    in_specs = (tok_spec, tok_spec, tok_spec, tok_spec, tok_spec, tok_spec, tok_spec, tok_spec, w_spec, w_spec, w_spec)
    out_specs = (tok_spec, tok_spec, grad_w_spec, grad_w_spec, grad_w_spec)
    return jax.shard_map(local_step, mesh=mesh, in_specs=in_specs, out_specs=out_specs, check_vma=False)
```

profile of v0, /device:TPU:103, one launch (start us, length us, event | category | flops | bytes accessed | tf_op | source)
XLA Modules:
  0.0 584.1 jit_solution(7455003262796135396)
XLA Ops:
  0.6 0.8 add_select_fusion
  1.8 0.8 copy.43
  2.6 1.5 convert_element_type.121
  4.1 3.9 multiply_convert_fusion
  8.0 13.9 %scatter_custom_fusion = bf16[2816,1024]{1,0:T(8,128)(2,1)} fusion(s32[2048]{0:T(1024)S(1)} %bitcast.184, bf16[2,256,8,1024]{3,2,1,0:T(8,128)(2,1)} %multiply_convert_fusion, bf16[]{:T(256)} %constant.13.clone.1), kind=kCustom, calls=%fused_computation.72 | custom fusion | bytes 9961984 | tf_op jit(solution)/shard_map/scatter | solution.py:46
  22.0 8.0 %all-to-all-start = ((bf16[32,1,88,1024]{3,2,1,0:T(8,128)(2,1)}), bf16[32,1,88,1024]{3,2,1,0:T(8,128)(2,1)}, u32[]{:S(2)}, u32[]{:S(2)}) async-start(bf16[32,1,88,1024]{3,2,1,0:T(8,128)(2,1)} %bitcast.179), calls=%async_computation | async-start | bytes 11534336 | tf_op jit(solution)/shard_map/all_to_all | solution.py:47
  30.2 13.9 %scatter_custom_fusion.1 = bf16[2816,1024]{1,0:T(8,128)(2,1)} fusion(s32[2048]{0:T(1024)S(1)} %bitcast.185, bf16[2,256,8,1024]{3,2,1,0:T(8,128)(2,1)} %multiply_convert_fusion, bf16[]{:T(256)} %constant.13.clone.1), kind=kCustom, calls=%fused_computation.70 | custom fusion | bytes 9961984 | tf_op jit(solution)/shard_map/scatter | solution.py:46
  44.2 64.0 %all-to-all-done = bf16[32,1,88,1024]{3,2,1,0:T(8,128)(2,1)} async-done(((bf16[32,1,88,1024]{3,2,1,0:T(8,128)(2,1)}), bf16[32,1,88,1024]{3,2,1,0:T(8,128)(2,1)}, u32[]{:S(2)}, u32[]{:S(2)}) %all-to-all-start) | async-done | bytes 5767200 | tf_op jit(solution)/shard_map/all_to_all | solution.py:47
  108.1 4.1 all-to-all-start.2
  112.3 0.7 copy.41
  113.0 0.8 copy.46
  114.3 8.6 %fusion.60 = f32[2,256,1,8]{3,2,1,0:T(1,128)S(1)} fusion(bf16[2,256,8,1024]{3,2,1,0:T(8,128)(2,1)} %param.14, bf16[2,256,1024,1]{2,1,0,3:T(8,128)(2,1)S(1)} %bitcast.182), kind=kOutput, calls=%fused_computation.87 | convolution fusion | flops 8388608 | bytes 9453568 | tf_op jit(solution)/shard_map/mtd,mtkd->mtk/dot_general | solution.py:37
  122.9 0.7 copy.53
  123.6 0.6 broadcast_clamp_fusion.1
  124.2 0.6 broadcast_clamp_fusion
  124.8 7.8 %convolution_convert_fusion.1 = bf16[2816,512]{1,0:T(8,128)(2,1)} fusion(bf16[2816,1024]{1,0:T(8,128)(2,1)} %bitcast.4, bf16[1,512,1024]{2,1,0:T(8,128)(2,1)} %param.23), kind=kOutput, calls=%fused_computation.68 | convolution fusion | flops 2954231808 | bytes 9699328 | tf_op jit(solution)/shard_map/erd,efd->erf/dot_general | solution.py:14
  132.6 57.0 %all-to-all-done.2 = bf16[32,1,88,1024]{3,2,1,0:T(8,128)(2,1)} async-done(((bf16[32,1,88,1024]{3,2,1,0:T(8,128)(2,1)}), bf16[32,1,88,1024]{3,2,1,0:T(8,128)(2,1)}, u32[]{:S(2)}, u32[]{:S(2)}) %all-to-all-start.2) | async-done | bytes 5767200 | tf_op jit(solution)/shard_map/all_to_all | solution.py:47
  189.6 11.8 %fusion.12 = (bf16[2816,512]{1,0:T(8,128)(2,1)S(1)}, bf16[2816,512]{1,0:T(8,128)(2,1)}) fusion(bf16[2,1,2816,512]{3,2,1,0:T(8,128)(2,1)} %param.20, bf16[2,1,2816,512]{3,2,1,0:T(8,128)(2,1)} %param.19, bf16[2816,1024]{1,0:T(8,128)(2,1)} %bitcast.17, bf16[1,512,1024]{2,1,0:T(8,128)(2,1)} %param.23), kind=kOutput, calls=%fused_computation.33 | convolution fusion | flops 2972975104 | bytes 18350080 | tf_op jit(solution)/shard_map/erd,efd->erf/dot_general | solution.py:14
  201.4 6.2 %fusion.70 = f32[2816,1024]{1,0:T(8,128)} fusion(bf16[2816,512]{1,0:T(8,128)(2,1)S(1)} %get-tuple-element.32, bf16[1,1024,512]{2,1,0:T(8,128)(2,1)S(1)} %copy-done), kind=kOutput, calls=%fused_computation.95 | convolution fusion | flops 2952790016 | bytes 15466496 | tf_op jit(solution)/shard_map/erf,edf->erd/dot_general | solution.py:21
  207.6 9.1 %fusion.43 = bf16[1,2816,1024]{2,1,0:T(8,128)(2,1)S(1)} fusion(f32[2816,1024]{1,0:T(8,128)} %fusion.70, bf16[1,1024,512]{2,1,0:T(8,128)(2,1)S(1)} %copy-done.7, bf16[2816,512]{1,0:T(8,128)(2,1)} %get-tuple-element.33, bf16[2,1,2816,512]{3,2,1,0:T(8,128)(2,1)S(1)} %bitcast.187), kind=kOutput, calls=%fused_computation.66 | convolution fusion | flops 2970091520 | bytes 24117248 | tf_op jit(solution)/shard_map/erf,edf->erd/dot_general | solution.py:22
  216.7 39.1 %copy.64 = bf16[1,2816,1024]{2,0,1:T(2,128)(2,1)} copy(bf16[1,2816,1024]{2,1,0:T(8,128)(2,1)S(1)} %fusion.43) | data formatting | bytes 11534336 | tf_op jit(solution)/shard_map/convert_element_type | solution.py:22
  256.3 34.8 %reduce.2 = bf16[2816,1024]{1,0:T(8,128)(2,1)} reduce(bf16[2816,1,1024]{2,1,0:T(2,128)(2,1)} %bitcast.174, bf16[]{:T(256)} %broadcast.108), dimensions={1}, to_apply=%bitcast.168.reduce_sub_computation | reduce | bytes 11534338
  291.2 12.3 %reshape.304 = bf16[32,2,45056]{2,1,0:T(2,128)(2,1)} reshape(bf16[2816,1024]{1,0:T(8,128)(2,1)} %reduce.2) | data formatting | bytes 11534336
  303.4 4.3 all-to-all-start.3
  307.8 12.6 %fusion.72 = f32[2816,1024]{1,0:T(8,128)} fusion(bf16[1,1024,512]{2,1,0:T(8,128)(2,1)S(1)} %copy-done, bf16[2816,512]{1,0:T(8,128)(2,1)} %convolution_convert_fusion.1, bf16[2,1,2816,512]{3,2,1,0:T(8,128)(2,1)} %param.20, bf16[2,1,2816,512]{3,2,1,0:T(8,128)(2,1)} %param.19), kind=kOutput, calls=%fused_computation.97 | convolution fusion | flops 2971533312 | bytes 21233664 | tf_op jit(solution)/shard_map/erf,edf->erd/dot_general | solution.py:21
  320.4 9.1 %fusion.42 = bf16[1,2816,1024]{2,1,0:T(8,128)(2,1)S(1)} fusion(f32[2816,1024]{1,0:T(8,128)} %fusion.72, bf16[1,1024,512]{2,1,0:T(8,128)(2,1)S(1)} %copy-done.8, bf16[2816,512]{1,0:T(8,128)(2,1)} %convolution_convert_fusion.1, bf16[2,1,2816,512]{3,2,1,0:T(8,128)(2,1)S(1)} %bitcast.189), kind=kOutput, calls=%fused_computation.65 | convolution fusion | flops 2970091520 | bytes 24117248 | tf_op jit(solution)/shard_map/erf,edf->erd/dot_general | solution.py:22
  329.5 39.1 %copy.65 = bf16[1,2816,1024]{2,0,1:T(2,128)(2,1)} copy(bf16[1,2816,1024]{2,1,0:T(8,128)(2,1)S(1)} %fusion.42) | data formatting | bytes 11534336 | tf_op jit(solution)/shard_map/convert_element_type | solution.py:22
  368.6 34.9 %reduce.3 = bf16[2816,1024]{1,0:T(8,128)(2,1)} reduce(bf16[2816,1,1024]{2,1,0:T(2,128)(2,1)} %bitcast.175, bf16[]{:T(256)} %broadcast.108), dimensions={1}, to_apply=%bitcast.169.reduce_sub_computation | reduce | bytes 11534338
  403.6 12.2 %reshape.306 = bf16[32,2,45056]{2,1,0:T(2,128)(2,1)} reshape(bf16[2816,1024]{1,0:T(8,128)(2,1)} %reduce.3) | data formatting | bytes 11534336
  415.8 6.2 %fusion.32 = f32[512,1024]{1,0:T(8,128)S(1)} fusion(bf16[2816,512]{1,0:T(8,128)(2,1)} %copy-done.9, bf16[2,1,2816,1024]{3,2,1,0:T(8,128)(2,1)} %param.18), kind=kOutput, calls=%fused_computation.55 | convolution fusion | flops 2952790016 | bytes 10747904 | tf_op jit(solution)/shard_map/erd,erf->edf/dot_general | solution.py:19
  422.0 8.4 %add_bitcast_fusion.2 = f32[1,1024,512]{1,2,0:T(8,128)S(1)} fusion(f32[512,1024]{1,0:T(8,128)S(1)} %fusion.32, bf16[2,1,2816,1024]{3,2,1,0:T(8,128)(2,1)} %param.18, bf16[2816,512]{1,0:T(8,128)(2,1)S(1)} %copy-done.10, bf16[2,1,2816,512]{3,2,1,0:T(8,128)(2,1)} %param.20, bf16[2,1,2816,512]{3,2,1,0:T(8,128)(2,1)} %param.19), kind=kOutput, calls=%fused_computation.91 | convolution fusion | flops 2972057600 | bytes 18612224 | tf_op jit(solution)/shard_map/erd,erf->edf/dot_general | solution.py:19
  430.5 6.8 %all-to-all-start.1 = ((bf16[32,2,45056]{2,1,0:T(2,128)(2,1)}), bf16[32,2,45056]{2,1,0:T(2,128)(2,1)}, u32[]{:S(2)}, u32[]{:S(2)}) async-start(bf16[32,2,45056]{2,1,0:T(2,128)(2,1)} %reshape.306), calls=%async_computation.1 | async-start | bytes 11534336 | tf_op jit(solution)/shard_map/all_to_all | solution.py:50
  437.3 9.0 %fusion.30 = f32[512,1024]{1,0:T(8,128)} fusion(bf16[2,1,2816,1024]{3,2,1,0:T(8,128)(2,1)} %param.18, bf16[2816,512]{1,0:T(8,128)(2,1)} %get-tuple-element.33, bf16[2,1,2816,512]{3,2,1,0:T(8,128)(2,1)} %param.19), kind=kOutput, calls=%fused_computation.53 | convolution fusion | flops 2964324352 | bytes 13631488 | tf_op jit(solution)/shard_map/erd,erf->edf/dot_general | solution.py:20
  446.3 1.8 copy.50
  448.1 8.3 %add_bitcast_fusion.1 = f32[1,1024,512]{1,2,0:T(8,128)S(1)} fusion(f32[512,1024]{1,0:T(8,128)} %fusion.30, bf16[2,1,2816,1024]{3,2,1,0:T(8,128)(2,1)} %param.18, bf16[2816,512]{1,0:T(8,128)(2,1)} %convolution_convert_fusion.1, bf16[2,1,2816,512]{3,2,1,0:T(8,128)(2,1)} %param.19), kind=kOutput, calls=%fused_computation.90 | convolution fusion | flops 2964848640 | bytes 15728640 | tf_op jit(solution)/shard_map/erd,erf->edf/dot_general | solution.py:20
  456.3 1.8 copy.51
  458.2 7.2 %fusion.48 = f32[512,1024]{1,0:T(8,128)S(1)} fusion(bf16[2816,1024]{1,0:T(8,128)(2,1)} %bitcast.17, bf16[2,1,2816,512]{3,2,1,0:T(8,128)(2,1)} %param.20, bf16[2,1,2816,512]{3,2,1,0:T(8,128)(2,1)} %param.19), kind=kOutput, calls=%fused_computation.77 | convolution fusion | flops 2964324352 | bytes 13631488 | tf_op jit(solution)/shard_map/erf,erd->efd/dot_general | solution.py:18
  465.4 9.0 %add_bitcast_fusion = f32[1,512,1024]{2,1,0:T(8,128)} fusion(f32[512,1024]{1,0:T(8,128)S(1)} %fusion.48, bf16[2816,1024]{1,0:T(8,128)(2,1)} %bitcast.4, bf16[2,1,2816,512]{3,2,1,0:T(8,128)(2,1)} %param.20, bf16[2,1,2816,512]{3,2,1,0:T(8,128)(2,1)} %param.19), kind=kOutput, calls=%fused_computation.89 | convolution fusion | flops 2964848640 | bytes 15728640 | tf_op jit(solution)/shard_map/erf,erd->efd/dot_general | solution.py:18
  474.4 21.4 %reshape.305 = bf16[2816,1,1024]{2,1,0:T(2,128)(2,1)} reshape(bf16[32,2,45056]{2,1,0:T(2,128)(2,1)} %all-to-all-done.3) | data formatting | bytes 11534336
  495.8 9.1 %copy.62 = bf16[1,2816,1024]{2,1,0:T(8,128)(2,1)} copy(bf16[1,2816,1024]{2,0,1:T(2,128)(2,1)} %bitcast.176) | data formatting | bytes 11534336
  504.9 10.2 %all-to-all-done.1 = bf16[32,2,45056]{2,1,0:T(2,128)(2,1)} async-done(((bf16[32,2,45056]{2,1,0:T(2,128)(2,1)}), bf16[32,2,45056]{2,1,0:T(2,128)(2,1)}, u32[]{:S(2)}, u32[]{:S(2)}) %all-to-all-start.1) | async-done | bytes 5767200 | tf_op jit(solution)/shard_map/all_to_all | solution.py:50
  515.1 21.1 %reshape.307 = bf16[2816,1,1024]{2,1,0:T(2,128)(2,1)} reshape(bf16[32,2,45056]{2,1,0:T(2,128)(2,1)} %all-to-all-done.1) | data formatting | bytes 11534336
  536.2 9.2 %copy.63 = bf16[1,2816,1024]{2,1,0:T(8,128)(2,1)} copy(bf16[1,2816,1024]{2,0,1:T(2,128)(2,1)} %bitcast.177) | data formatting | bytes 11534336
  545.4 14.4 %gather_fusion.1 = bf16[2048,1024]{1,0:T(8,128)(2,1)} fusion(bf16[2816,1024]{1,0:T(8,128)(2,1)} %bitcast.172, s32[2048]{0:T(1024)S(1)} %copy-done.3), kind=kCustom, calls=%fused_computation.1.clone | custom fusion | bytes 8396800 | tf_op jit(solution)/shard_map/jit(_take)/gather | solution.py:51
  559.8 4.1 fusion.46
  564.0 14.4 %gather_fusion = bf16[2048,1024]{1,0:T(8,128)(2,1)} fusion(bf16[2816,1024]{1,0:T(8,128)(2,1)} %bitcast.173, s32[2048]{0:T(1024)S(1)} %copy-done.2), kind=kCustom, calls=%fused_computation.clone | custom fusion | bytes 8396800 | tf_op jit(solution)/shard_map/jit(_take)/gather | solution.py:51
  578.4 4.1 fusion.47
  582.6 1.1 pad_maximum_fusion
  (47 shorter events, 1.6 us)
Async XLA Ops:
  0.6 200.8 %copy-start = (bf16[1,1024,512]{2,1,0:T(8,128)(2,1)S(1)}, bf16[1,1024,512]{2,1,0:T(8,128)(2,1)}, u32[]{:S(2)}) copy-start(bf16[1,1024,512]{2,1,0:T(8,128)(2,1)} %param.21) | copy-start | bytes 3145732
  22.0 86.2 %all-to-all-start = ((bf16[32,1,88,1024]{3,2,1,0:T(8,128)(2,1)}), bf16[32,1,88,1024]{3,2,1,0:T(8,128)(2,1)}, u32[]{:S(2)}, u32[]{:S(2)}) async-start(bf16[32,1,88,1024]{3,2,1,0:T(8,128)(2,1)} %bitcast.179), calls=%async_computation | async-start | bytes 11534336 | tf_op jit(solution)/shard_map/all_to_all | solution.py:47
  108.1 6.1 %copy-start.4 = (bf16[2,256,1024]{2,1,0:T(8,128)(2,1)S(1)}, bf16[2,256,1024]{2,1,0:T(8,128)(2,1)}, u32[]{:S(2)}) copy-start(bf16[2,256,1024]{2,1,0:T(8,128)(2,1)} %param.13) | copy-start | bytes 3145732
  108.1 81.5 %all-to-all-start.2 = ((bf16[32,1,88,1024]{3,2,1,0:T(8,128)(2,1)}), bf16[32,1,88,1024]{3,2,1,0:T(8,128)(2,1)}, u32[]{:S(2)}, u32[]{:S(2)}) async-start(bf16[32,1,88,1024]{3,2,1,0:T(8,128)(2,1)} %bitcast.178), calls=%async_computation.2 | async-start | bytes 11534336 | tf_op jit(solution)/shard_map/all_to_all | solution.py:47
  124.8 82.8 %slice-start = ((s8[5767168]{0:T(1024)(128)(4,1)}), s8[1572864]{0:T(1024)(128)(4,1)S(1)}, s32[]{:S(2)}) async-start(s8[5767168]{0:T(1024)(128)(4,1)} %bitcast.186), calls=%async_computation.4 | async-start | bytes 3145728
  189.6 18.0 %slice-start.1 = ((s8[5767168]{0:T(1024)(128)(4,1)}), s8[4194304]{0:T(1024)(128)(4,1)S(1)}, s32[]{:S(2)}) async-start(s8[5767168]{0:T(1024)(128)(4,1)} %bitcast.186), calls=%async_computation.5 | async-start | bytes 8388608
  201.4 6.2 %copy-start.9 = (bf16[2816,512]{1,0:T(8,128)(2,1)}, bf16[2816,512]{1,0:T(8,128)(2,1)S(1)}, u32[]{:S(2)}) copy-start(bf16[2816,512]{1,0:T(8,128)(2,1)S(1)} %get-tuple-element.32) | copy-start | bytes 8650756
  201.4 6.2 %copy-start.7 = (bf16[1,1024,512]{2,1,0:T(8,128)(2,1)S(1)}, bf16[1,1024,512]{2,1,0:T(8,128)(2,1)}, u32[]{:S(2)}) copy-start(bf16[1,1024,512]{2,1,0:T(8,128)(2,1)} %param.22) | copy-start | bytes 3145732
  303.4 17.0 %slice-start.2 = ((s8[5767168]{0:T(1024)(128)(4,1)}), s8[1572864]{0:T(1024)(128)(4,1)S(1)}, s32[]{:S(2)}) async-start(s8[5767168]{0:T(1024)(128)(4,1)} %bitcast.188), calls=%async_computation.6 | async-start | bytes 3145728
  303.4 127.1 %all-to-all-start.3 = ((bf16[32,2,45056]{2,1,0:T(2,128)(2,1)}), bf16[32,2,45056]{2,1,0:T(2,128)(2,1)}, u32[]{:S(2)}, u32[]{:S(2)}) async-start(bf16[32,2,45056]{2,1,0:T(2,128)(2,1)} %reshape.304), calls=%async_computation.3 | async-start | bytes 11534336 | tf_op jit(solution)/shard_map/all_to_all | solution.py:50
  307.7 12.6 %slice-start.3 = ((s8[5767168]{0:T(1024)(128)(4,1)}), s8[4194304]{0:T(1024)(128)(4,1)S(1)}, s32[]{:S(2)}) async-start(s8[5767168]{0:T(1024)(128)(4,1)} %bitcast.188), calls=%async_computation.7 | async-start | bytes 8388608
  307.8 12.6 %copy-start.8 = (bf16[1,1024,512]{2,1,0:T(8,128)(2,1)S(1)}, bf16[1,1024,512]{2,1,0:T(8,128)(2,1)}, u32[]{:S(2)}) copy-start(bf16[1,1024,512]{2,1,0:T(8,128)(2,1)} %param.22) | copy-start | bytes 3145732
  415.8 6.2 %copy-start.10 = (bf16[2816,512]{1,0:T(8,128)(2,1)S(1)}, bf16[2816,512]{1,0:T(8,128)(2,1)}, u32[]{:S(2)}) copy-start(bf16[2816,512]{1,0:T(8,128)(2,1)} %convolution_convert_fusion.1) | copy-start | bytes 8650756
  430.5 84.6 %all-to-all-start.1 = ((bf16[32,2,45056]{2,1,0:T(2,128)(2,1)}), bf16[32,2,45056]{2,1,0:T(2,128)(2,1)}, u32[]{:S(2)}, u32[]{:S(2)}) async-start(bf16[32,2,45056]{2,1,0:T(2,128)(2,1)} %reshape.306), calls=%async_computation.1 | async-start | bytes 11534336 | tf_op jit(solution)/shard_map/all_to_all | solution.py:50
  536.2 9.2 %copy-start.3 = (s32[2048]{0:T(1024)S(1)}, s32[2048]{0:T(1024)}, u32[]{:S(2)}) copy-start(s32[2048]{0:T(1024)} %broadcast_clamp_fusion) | copy-start | bytes 24580
  545.4 14.4 %copy-start.6 = (pred[256,8]{1,0:T(8,128)(4,1)S(1)}, pred[256,8]{1,0:T(8,128)(4,1)}, u32[]{:S(2)}) copy-start(pred[256,8]{1,0:T(8,128)(4,1)} %copy.46) | copy-start | bytes 6148
  545.4 18.5 %copy-start.2 = (s32[2048]{0:T(1024)S(1)}, s32[2048]{0:T(1024)}, u32[]{:S(2)}) copy-start(s32[2048]{0:T(1024)} %broadcast_clamp_fusion.1) | copy-start | bytes 24580
  563.9 14.5 %copy-start.5 = (pred[256,8]{1,0:T(8,128)(4,1)S(1)}, pred[256,8]{1,0:T(8,128)(4,1)}, u32[]{:S(2)}) copy-start(pred[256,8]{1,0:T(8,128)(4,1)} %copy.41) | copy-start | bytes 6148
  563.9 19.7 %copy-start.1 = (bf16[1,1024,512]{2,1,0:T(8,128)(2,1)S(1)}, bf16[1,1024,512]{2,1,0:T(8,128)(2,1)}, u32[]{:S(2)}) copy-start(bf16[1,1024,512]{2,1,0:T(8,128)(2,1)} %param.21) | copy-start | bytes 3145732
where the time goes:
time: 595 us; the launch traced here: 584 us
  local copies, waits for them, and re-layouts  228 us (38%)
  waiting for transfers between devices  131 us (22%)
  matrix products  113 us (19%)
  other arithmetic  86.6 us (15%)
  starting transfers between devices  23.2 us (4%)
    all_to_all x2, waiting for transfers between devices, local_step(): lax.all_to_all(send_buf.reshape(group_size, local_exp, capacity, d_model)...  121 us
    unnamed x40, local copies, waits for them, and re-layouts  90.3 us
    convert_element_type x2, local copies, waits for them, and re-layouts, expert_grads(): (dx_rows + jnp.einsum('erf,edf->erd', grad_h3, w_up, preferred_element_ty...  78.2 us
    unnamed x4, other arithmetic  69.8 us
    gather x2, local copies, waits for them, and re-layouts, local_step(): jnp.take(returned.reshape(experts * capacity, d_model), send_rows[micro_i...  28.8 us
    scatter x2, local copies, waits for them, and re-layouts, local_step(): send_buf.at[send_rows[micro_idx].reshape(-1)]  27.9 us
    dot_general x2, matrix products, expert_grads(): jnp.einsum('erd,efd->erf', dy_rows, w_down, preferred_element_type=jnp.fl...  19.6 us
    dot_general x2, matrix products, expert_grads(): jnp.einsum('erf,edf->erd', grad_h1, w_gate, preferred_element_type=jnp.fl...  18.8 us
  transfers between devices with their start and end apart: 4, of which 3 were waited for; matrix products, arithmetic and copies ran while one was open for 38% of the time, Pallas kernels for 0%

commit v1 on v0

v1 whole, which is shorter than its diff:
```python
import functools
import jax
import jax.numpy as jnp
from jax import lax
from jax.experimental import pallas as pl
from jax.experimental.pallas import tpu as pltpu
from jax.sharding import PartitionSpec as P

F32 = jnp.float32
BF16 = jnp.bfloat16


def dot_nn(a, b):
    return lax.dot_general(a, b, (((1,), (0,)), ((), ())), preferred_element_type=F32)


def dot_nt(a, b):
    return lax.dot_general(a, b, (((1,), (1,)), ((), ())), preferred_element_type=F32)


def dot_tn(a, b):
    return lax.dot_general(a, b, (((0,), (0,)), ((), ())), preferred_element_type=F32)


def gather_rows(pos, gate, dy, rows):
    tokens = pos.shape[1]
    hit = lax.broadcasted_iota(jnp.int32, (rows, tokens), 0).astype(F32) == pos
    gate_col = jnp.sum(jnp.where(hit, gate, 0.0), axis=1, keepdims=True)
    onehot = jnp.where(hit, 1.0, 0.0).astype(BF16)
    return (dot_nn(onehot, dy) * gate_col).astype(BF16)


def swiglu_grads(dyd, h1, h3, w2):
    h1 = h1.astype(F32)
    h3 = h3.astype(F32)
    sig = jax.nn.sigmoid(h1)
    silu = h1 * sig
    act = (silu * h3).astype(BF16)
    da = dot_nt(dyd, w2).astype(BF16).astype(F32)
    dh1 = (da * h3 * sig * (1.0 + h1 * (1.0 - sig))).astype(BF16)
    dh3 = (da * silu).astype(BF16)
    return act, dh1, dh3


def expert_kernel(first, pos, gate, dy, x, h1, h3, w1, w3, w2, *refs):
    if first:
        dx, g1, g3, g2 = refs
    else:
        p1, p3, p2, dx, g1, g3, g2 = refs
    rows = x.shape[0]
    dyd = gather_rows(pos[0], gate[0], dy[0], rows)
    act, dh1, dh3 = swiglu_grads(dyd, h1[...], h3[...], w2[...])
    dx[...] = (dot_nt(dh1, w1[...]) + dot_nt(dh3, w3[...])).astype(BF16)

    @pl.when(pl.program_id(0) == 0)
    def _():
        for k, g in enumerate((g1, g3, g2)):
            g[...] = jnp.zeros_like(g) if first else (p1, p3, p2)[k][...]

    g1[...] += dot_tn(x[...], dh1)
    g3[...] += dot_tn(x[...], dh3)
    g2[...] += dot_tn(act, dyd)


def expert_call(pos, gate, dy, x, h1, h3, w1, w3, w2, prev):
    units, tokens, d = dy.shape
    f = h1.shape[1]
    rows = x.shape[0] // units
    whole = lambda a, b: pl.BlockSpec((a, b), lambda i: (0, 0))
    in_specs = [pl.BlockSpec((1, 1, tokens), lambda i: (i, 0, 0))] * 2 + [
        pl.BlockSpec((1, tokens, d), lambda i: (i, 0, 0)),
        pl.BlockSpec((rows, d), lambda i: (i, 0)),
        pl.BlockSpec((rows, f), lambda i: (i, 0)),
        pl.BlockSpec((rows, f), lambda i: (i, 0)),
        whole(d, f), whole(d, f), whole(f, d)]
    args = [pos, gate, dy, x, h1, h3, w1, w3, w2]
    if prev is not None:
        in_specs += [whole(d, f), whole(d, f), whole(f, d)]
        args += list(prev)
    return pl.pallas_call(
        functools.partial(expert_kernel, prev is None),
        grid=(units,),
        in_specs=in_specs,
        out_specs=[pl.BlockSpec((rows, d), lambda i: (i, 0)), whole(d, f), whole(d, f), whole(f, d)],
        out_shape=[jax.ShapeDtypeStruct(x.shape, BF16), jax.ShapeDtypeStruct((d, f), F32), jax.ShapeDtypeStruct((d, f), F32), jax.ShapeDtypeStruct((f, d), F32)],
        compiler_params=pltpu.CompilerParams(dimension_semantics=('arbitrary',), vmem_limit_bytes=56 * 2**20),
        cost_estimate=pl.CostEstimate(flops=15 * 2 * x.shape[0] * d * f, bytes_accessed=60 * 2**20, transcendentals=0),
        name='expert')(*args)


def combine_kernel(idx, rows_ref, out, acc):
    u = pl.program_id(0)
    rows = rows_ref.shape[0]
    tokens = idx.shape[0]
    want = lax.broadcasted_iota(jnp.int32, (tokens, rows), 1) + u * rows
    hit = want == idx[:, 0:1]
    for j in range(1, idx.shape[1]):
        hit = hit | (want == idx[:, j:j + 1])
    part = dot_nn(jnp.where(hit, 1.0, 0.0).astype(BF16), rows_ref[...])

    @pl.when(u == 0)
    def _():
        acc[...] = part

    @pl.when(u > 0)
    def _():
        acc[...] += part

    @pl.when(u == pl.num_programs(0) - 1)
    def _():
        out[...] = acc[...].astype(BF16)


def combine_call(idx, rows, units):
    tokens, d = idx.shape[0], rows.shape[1]
    step = rows.shape[0] // units
    return pl.pallas_call(
        combine_kernel,
        grid=(units,),
        in_specs=[pl.BlockSpec(idx.shape, lambda i: (0, 0)), pl.BlockSpec((step, d), lambda i: (i, 0))],
        out_specs=pl.BlockSpec((tokens, d), lambda i: (0, 0)),
        out_shape=jax.ShapeDtypeStruct((tokens, d), BF16),
        scratch_shapes=[pltpu.VMEM((tokens, d), F32)],
        compiler_params=pltpu.CompilerParams(dimension_semantics=('arbitrary',)),
        cost_estimate=pl.CostEstimate(flops=2 * tokens * rows.shape[0] * d, bytes_accessed=8 * 2**20, transcendentals=0),
        name='combine')(idx, rows)


def solution(mesh):
    group = mesh.shape['ep']
    tok_spec = P(None, ('dp', 'ep'))
    w_spec = P('ep')
    grad_w_spec = P(('dp', 'ep'))

    def local_step(grad_out, expert_out, gate_vals, topk_idx, slot_idx, x_dispatch, h1_pre, h3_pre, w_gate, w_up, w_down):
        n_micro, tokens, top_k, d = expert_out.shape
        experts = group * w_gate.shape[0]
        capacity = x_dispatch.shape[2] // group
        units = group // 2
        me = lax.axis_index('ep')

        all_dy = [lax.all_gather(grad_out[m], 'ep', axis=0).reshape(units, 2 * tokens, d) for m in range(n_micro)]

        idx_t = jnp.swapaxes(topk_idx, 1, 2)[:, :, None, :]
        slot_t = jnp.swapaxes(slot_idx, 1, 2)[:, :, None, :]
        gate_t = jnp.swapaxes(gate_vals, 1, 2)[:, :, None, :]
        match = idx_t == jnp.arange(experts, dtype=jnp.int32)[None, None, :, None]
        slot_map = jnp.max(jnp.where(match, slot_t, -1), axis=1)
        pos_map = jnp.where(slot_map >= 0, slot_map + capacity * lax.rem(me, 2), -1).astype(F32)
        gate_map = jnp.sum(jnp.where(match, gate_t, 0.0), axis=1)
        maps = jnp.stack([pos_map, gate_map], axis=1)
        maps = jnp.moveaxis(maps, 2, 0).reshape(experts, 2 * n_micro, tokens)
        maps = lax.all_to_all(maps, 'ep', 0, 0, tiled=True)
        maps = jnp.moveaxis(maps, 1, 0).reshape(n_micro, 2, units, 1, 2 * tokens)
        send_rows = jnp.where(slot_idx >= 0, topk_idx * capacity + slot_idx, -1)

        grad_gate = jnp.sum(grad_out[:, :, None, :].astype(F32) * expert_out.astype(F32), axis=-1)

        prev = None
        dx = []
        for m in range(n_micro):
            rows, g1, g3, g2 = expert_call(maps[m, 0], maps[m, 1], all_dy[m], x_dispatch[m, 0], h1_pre[m, 0], h3_pre[m, 0], w_gate[0], w_up[0], w_down[0], prev)
            prev = (g1, g3, g2)
            back = lax.all_to_all(rows.reshape(group, capacity, d), 'ep', 0, 0, tiled=True)
            dx.append(combine_call(send_rows[m], back.reshape(experts * capacity, d), units))
        return jnp.stack(dx), grad_gate, prev[0][None], prev[1][None], prev[2][None]

    in_specs = (tok_spec, tok_spec, tok_spec, tok_spec, tok_spec, tok_spec, tok_spec, tok_spec, w_spec, w_spec, w_spec)
    out_specs = (tok_spec, tok_spec, grad_w_spec, grad_w_spec, grad_w_spec)
    return jax.shard_map(local_step, mesh=mesh, in_specs=in_specs, out_specs=out_specs, check_vma=False)
```

time: 595 us -> 385 us (0.65); the launches traced: 584 us -> 384 us
  local copies, waits for them, and re-layouts: 228 us -> 23.9 us
  Pallas kernels: 0 us -> 127 us
  matrix products: 113 us -> 0 us
  other arithmetic: 86.6 us -> 9.12 us
  blocking collectives: 0 us -> 74.5 us
  between operations: 1.39 us -> 14.2 us
  waiting for transfers between devices: 131 us -> 120 us
  starting transfers between devices: 23.2 us -> 15.4 us
    pallas_call x0 -> x4, Pallas kernels: none -> 127 us  [the longest x2 95 us: expert_call(): pl.pallas_call(functools.partial(expert_kernel, prev is None), grid=(unit...]
    dot_general x13 -> x0, matrix products: 113 us -> none  [the longest x2 19.6 us: expert_grads(): jnp.einsum('erd,efd->erf', dy_rows, w_down, preferred_element_type=jnp.fl...]
    unnamed x40 -> x10, local copies, waits for them, and re-layouts: 90.3 us -> 0.84 us
    convert_element_type x2 -> x0, local copies, waits for them, and re-layouts: 78.2 us -> none  [expert_grads(): (dx_rows + jnp.einsum('erf,edf->erd', grad_h3, w_up, preferred_element_ty...]
    all_to_all x4 -> x2, waiting for transfers between devices: 131 us -> 55.1 us  [the longest x1 55.1 us: local_step(): lax.all_to_all(rows.reshape(group, capacity, d), 'ep', 0, 0, tiled=True)]
    all_to_all x0 -> x1, blocking collectives: none -> 74.5 us  [local_step(): lax.all_to_all(rows.reshape(group, capacity, d), 'ep', 0, 0, tiled=True)]
    unnamed x4 -> x0, other arithmetic: 69.8 us -> none
    all_gather x0 -> x2, waiting for transfers between devices: none -> 64.3 us  [local_step(): lax.all_gather(grad_out[m], 'ep', axis=0).reshape(units, 2 * tokens, d)]
  transfers between devices with their start and end apart: 4 -> 4, of which waited for: 3 -> 3; matrix products, arithmetic and copies ran while one was open for 38% -> 7% of each run, Pallas kernels for 0% -> 16%
where the time goes in v1:
time: 385 us; the launch traced here: 384 us
  Pallas kernels  127 us (33%)
  waiting for transfers between devices  120 us (31%)
  blocking collectives  74.5 us (19%)
  local copies, waits for them, and re-layouts  23.9 us (6%)
  starting transfers between devices  15.4 us (4%)
  between operations  14.2 us (4%)
  other arithmetic  9.12 us (2%)
    pallas_call x2, Pallas kernels, expert_call(): pl.pallas_call(functools.partial(expert_kernel, prev is None), grid=(unit...  95 us
    all_to_all x1, blocking collectives, local_step(): lax.all_to_all(rows.reshape(group, capacity, d), 'ep', 0, 0, tiled=True)  74.5 us
    all_gather x2, waiting for transfers between devices, local_step(): lax.all_gather(grad_out[m], 'ep', axis=0).reshape(units, 2 * tokens, d)  64.3 us
    all_to_all x1, waiting for transfers between devices, local_step(): lax.all_to_all(rows.reshape(group, capacity, d), 'ep', 0, 0, tiled=True)  55.1 us
    pallas_call x2, Pallas kernels, combine_call(): pl.pallas_call(combine_kernel, grid=(units,), in_specs=[pl.BlockSpec(idx....  31.6 us
    squeeze x1, local copies, waits for them, and re-layouts, local_step(): x_dispatch[m, 0]  9.89 us
    squeeze x1, local copies, waits for them, and re-layouts, local_step(): h3_pre[m, 0]  8.34 us
    all_to_all x1, starting transfers between devices, local_step(): maps = lax.all_to_all(maps, 'ep', 0, 0, tiled=True)  7.99 us
  transfers between devices with their start and end apart: 4, of which 3 were waited for; matrix products, arithmetic and copies ran while one was open for 7% of the time, Pallas kernels for 16%

profile of v1, /device:TPU:103, one launch (start us, length us, event | category | flops | bytes accessed | tf_op | source)
XLA Modules:
  0.0 383.8 jit_solution(3664201502432714259)
XLA Ops:
  7.2 0.1 all-gather.3.cloned.1.call-start
  7.2 2.2 fusion
  9.5 0.1 all-gather.3.cloned.1.call-update
  9.5 0.1 all-gather.5.cloned.1.call-start
  9.6 0.7 all-gather.5.cloned.1.call-update
  10.4 0.8 select_reduce_fusion.1
  11.2 0.8 select_reduce_fusion
  12.0 0.7 copy.48
  12.8 8.0 %all-to-all-start = ((f32[32,4,256]{2,1,0:T(4,128)}), f32[32,4,256]{2,1,0:T(4,128)S(1)}, u32[]{:S(2)}, u32[]{:S(2)}) async-start(f32[32,4,256]{2,1,0:T(4,128)} %copy.48), calls=%async_computation | async-start | bytes 262144 | tf_op jit(solution)/shard_map/all_to_all | solution.py:153
  20.8 9.9 %slice_bitcast_fusion.1 = (bf16[2816,1024]{1,0:T(8,128)(2,1)}, bf16[2816,1024]{1,0:T(8,128)(2,1)}) fusion(bf16[2,1,2816,1024]{3,2,1,0:T(8,128)(2,1)} %param.16), kind=kLoop, calls=%fused_computation.2 | loop fusion | bytes 23068672 | tf_op jit(solution)/shard_map/squeeze | solution.py:162
  30.7 8.3 %slice_bitcast_fusion.4 = (bf16[2816,512]{1,0:T(8,128)(2,1)}, bf16[2816,512]{1,0:T(8,128)(2,1)}, bf16[2816,512]{1,0:T(8,128)(2,1)}, bf16[2816,512]{1,0:T(8,128)(2,1)}) fusion(bf16[2,1,2816,512]{3,2,1,0:T(8,128)(2,1)} %param.18, bf16[2,1,2816,512]{3,2,1,0:T(8,128)(2,1)} %param.17), kind=kLoop, calls=%fused_computation.5 | loop fusion | bytes 23068672 | tf_op jit(solution)/shard_map/squeeze | solution.py:162
  39.0 0.0 all-to-all-done
  39.0 0.1 reshape.63
  39.2 0.7 slice_bitcast_fusion.10
  39.8 41.4 %all-gather.3.cloned.1.call-done = bf16[32,256,1024]{2,1,0:T(8,128)(2,1)} async-done(((bf16[1,256,1024]{2,1,0:T(8,128)(2,1)}), bf16[32,256,1024]{2,1,0:T(8,128)(2,1)}) %all-gather.3.cloned.1.call-update) | async-done | bytes 16777232 | tf_op jit(solution)/shard_map/all_gather | solution.py:142
  81.2 46.5 %expert.2 = (bf16[2816,1024]{1,0:T(8,128)(2,1)}, f32[1024,512]{1,0:T(8,128)}, f32[1024,512]{1,0:T(8,128)}, f32[512,1024]{1,0:T(8,128)}) custom-call(f32[16,1,512]{2,1,0:T(1,128)} %get-tuple-element.54.pos, f32[16,1,512]{2,1,0:T(1,128)} %get-tuple-element.51.gate, bf16[16,512,1024]{2,1,0:T(8,128)(2,1)} %bitcast.61, bf16[2816,1024]{1,0:T(8,128)(2,1)} %get-tuple-element.41.x, ...), custom_call_target="tpu_custom_call" | custom-call | flops 44291850240 | bytes 62914560 | tf_op jit(solution)/shard_map/expert/pallas_call | solution.py:80
  127.7 22.9 %all-gather.5.cloned.1.call-done = bf16[32,256,1024]{2,1,0:T(8,128)(2,1)} async-done(((bf16[1,256,1024]{2,1,0:T(8,128)(2,1)}), bf16[32,256,1024]{2,1,0:T(8,128)(2,1)}) %all-gather.5.cloned.1.call-update) | async-done | bytes 16777232 | tf_op jit(solution)/shard_map/all_gather | solution.py:142
  150.6 48.6 %expert.3 = (bf16[2816,1024]{1,0:T(8,128)(2,1)}, f32[1024,512]{1,0:T(8,128)}, f32[1024,512]{1,0:T(8,128)}, f32[512,1024]{1,0:T(8,128)}) custom-call(f32[16,1,512]{2,1,0:T(1,128)} %get-tuple-element.53.pos, f32[16,1,512]{2,1,0:T(1,128)} %get-tuple-element.52.gate, bf16[16,512,1024]{2,1,0:T(8,128)(2,1)} %bitcast.60, bf16[2816,1024]{1,0:T(8,128)(2,1)} %get-tuple-element.42.x, ...), custom_call_target="tpu_custom_call" | custom-call | flops 44291850240 | bytes 62914560 | tf_op jit(solution)/shard_map/expert/pallas_call | solution.py:80
  199.2 74.5 %all_to_all.15 = bf16[32,88,1024]{2,1,0:T(8,128)(2,1)} all-to-all(bf16[32,88,1024]{2,1,0:T(8,128)(2,1)} %bitcast.50), channel_id=1, replica_groups=mesh['dp'=1,'ep'=32] {'ep'}, dimensions={0} | all-to-all | bytes 11534336 | tf_op jit(solution)/shard_map/all_to_all | solution.py:164
  273.6 0.0 copy-start.2
  273.6 0.0 copy-start
  273.6 0.0 copy-start.3
  273.6 7.3 %all-to-all-start.1 = ((bf16[32,88,1024]{2,1,0:T(8,128)(2,1)}), bf16[32,88,1024]{2,1,0:T(8,128)(2,1)}, u32[]{:S(2)}, u32[]{:S(2)}) async-start(bf16[32,88,1024]{2,1,0:T(8,128)(2,1)} %bitcast.49), calls=%async_computation.1 | async-start | bytes 11534336 | tf_op jit(solution)/shard_map/all_to_all | solution.py:164
  280.9 0.0 copy-done.2
  280.9 0.1 copy.45
  281.0 0.0 copy-done
  281.0 0.2 convert_element_type.22
  281.3 0.0 copy-done.3
  281.3 0.1 copy.44
  281.5 0.2 copy.46
  281.6 5.1 %multiply_reduce_fusion = f32[2,256,8]{2,1,0:T(8,128)S(1)} fusion(bf16[2,256,8,1024]{3,2,1,0:T(8,128)(2,1)} %param.12, f32[2,256,1024]{2,1,0:T(8,128)S(1)} %convert_element_type.22), kind=kLoop, calls=%fused_computation | loop fusion | flops 12578816 | bytes 10502144 | tf_op jit(solution)/shard_map/reduce_sum | solution.py:157
  286.7 0.7 copy.50
  287.5 0.7 slice_bitcast_fusion.7
  288.2 15.8 %combine.3 = bf16[256,1024]{1,0:T(8,128)(2,1)} custom-call(s32[256,8]{1,0:T(8,128)} %get-tuple-element.50.idx, bf16[2816,1024]{1,0:T(8,128)(2,1)} %bitcast.48), custom_call_target="tpu_custom_call" | custom-call | flops 1476395008 | bytes 8388608 | tf_op jit(solution)/shard_map/combine/pallas_call | solution.py:117
  304.0 0.0 copy-start.1
  304.0 55.1 %all-to-all-done.1 = bf16[32,88,1024]{2,1,0:T(8,128)(2,1)} async-done(((bf16[32,88,1024]{2,1,0:T(8,128)(2,1)}), bf16[32,88,1024]{2,1,0:T(8,128)(2,1)}, u32[]{:S(2)}, u32[]{:S(2)}) %all-to-all-start.1) | async-done | bytes 5767200 | tf_op jit(solution)/shard_map/all_to_all | solution.py:164
  359.0 15.8 %combine.2 = bf16[256,1024]{1,0:T(8,128)(2,1)} custom-call(s32[256,8]{1,0:T(8,128)} %get-tuple-element.49.idx, bf16[2816,1024]{1,0:T(8,128)(2,1)} %bitcast.19.rows_ref), custom_call_target="tpu_custom_call" | custom-call | flops 1476395008 | bytes 8388608 | tf_op jit(solution)/shard_map/combine/pallas_call | solution.py:117
  374.8 0.0 copy-done.1
  374.8 2.1 pad_maximum_fusion
  (7 shorter events, 0.1 us)
Async XLA Ops:
  7.2 74.0 %all-gather.3.cloned.1.call-start = ((), (), s32[]{:S(2)}) async-start(), calls=%async_computation.3 | async-start | bytes 17301504 | tf_op jit(solution)/shard_map/all_gather | solution.py:142
  9.5 141.1 %all-gather.5.cloned.1.call-start = ((), (), s32[]{:S(2)}) async-start(), calls=%async_computation.4 | async-start | bytes 17301504 | tf_op jit(solution)/shard_map/all_gather | solution.py:142
  12.8 26.2 %all-to-all-start = ((f32[32,4,256]{2,1,0:T(4,128)}), f32[32,4,256]{2,1,0:T(4,128)S(1)}, u32[]{:S(2)}, u32[]{:S(2)}) async-start(f32[32,4,256]{2,1,0:T(4,128)} %copy.48), calls=%async_computation | async-start | bytes 262144 | tf_op jit(solution)/shard_map/all_to_all | solution.py:153
  273.6 7.3 %copy-start.2 = (s32[2,256,8]{1,2,0:T(8,128)S(1)}, s32[2,256,8]{1,2,0:T(8,128)}, u32[]{:S(2)}) copy-start(s32[2,256,8]{1,2,0:T(8,128)} %param.15) | copy-start | bytes 49156
  273.6 7.4 %copy-start = (bf16[2,256,1024]{2,1,0:T(8,128)(2,1)S(1)}, bf16[2,256,1024]{2,1,0:T(8,128)(2,1)}, u32[]{:S(2)}) copy-start(bf16[2,256,1024]{2,1,0:T(8,128)(2,1)} %param.11) | copy-start | bytes 3145732
  273.6 7.7 %copy-start.3 = (s32[2,256,8]{1,2,0:T(8,128)S(1)}, s32[2,256,8]{1,2,0:T(8,128)}, u32[]{:S(2)}) copy-start(s32[2,256,8]{1,2,0:T(8,128)} %param.14) | copy-start | bytes 49156
  273.6 85.4 %all-to-all-start.1 = ((bf16[32,88,1024]{2,1,0:T(8,128)(2,1)}), bf16[32,88,1024]{2,1,0:T(8,128)(2,1)}, u32[]{:S(2)}, u32[]{:S(2)}) async-start(bf16[32,88,1024]{2,1,0:T(8,128)(2,1)} %bitcast.49), calls=%async_computation.1 | async-start | bytes 11534336 | tf_op jit(solution)/shard_map/all_to_all | solution.py:164
  304.0 70.9 %copy-start.1 = (bf16[256,1024]{1,0:T(8,128)(2,1)S(1)}, bf16[256,1024]{1,0:T(8,128)(2,1)}, u32[]{:S(2)}) copy-start(bf16[256,1024]{1,0:T(8,128)(2,1)} %combine.3) | copy-start | bytes 1572868
Sparse Core Ops, SparseCore 0:
  10.7 70.4 all-gather.2
  83.9 66.6 all-gather.4

commit v2 on v0

v2 whole, which is shorter than its diff:
```python
import functools
import jax
import jax.numpy as jnp
from jax import lax
from jax.experimental import pallas as pl
from jax.experimental.pallas import tpu as pltpu
from jax.sharding import PartitionSpec as P

F32 = jnp.float32
BF16 = jnp.bfloat16
MESH = pl.DeviceIdType.MESH
SIDE = 4
ORDER = ((0, 0), (1, 0), (3, 0), (0, 1), (0, 3), (1, 1), (3, 3), (1, 3), (3, 1), (2, 0), (0, 2), (2, 1), (1, 2), (2, 3), (3, 2), (2, 2))
UNITS = len(ORDER)


def dot_nn(a, b):
    return lax.dot_general(a, b, (((1,), (0,)), ((), ())), preferred_element_type=F32)


def dot_nt(a, b):
    return lax.dot_general(a, b, (((1,), (1,)), ((), ())), preferred_element_type=F32)


def dot_tn(a, b):
    return lax.dot_general(a, b, (((0,), (0,)), ((), ())), preferred_element_type=F32)


def gather_rows(pos, gate, dy, rows):
    tokens = pos.shape[1]
    hit = lax.broadcasted_iota(jnp.int32, (rows, tokens), 0).astype(F32) == pos
    gate_col = jnp.sum(jnp.where(hit, gate, 0.0), axis=1, keepdims=True)
    onehot = jnp.where(hit, 1.0, 0.0).astype(BF16)
    return (dot_nn(onehot, dy) * gate_col).astype(BF16)


def swiglu_grads(dyd, h1, h3, w2):
    h1 = h1.astype(F32)
    h3 = h3.astype(F32)
    sig = jax.nn.sigmoid(h1)
    silu = h1 * sig
    act = (silu * h3).astype(BF16)
    da = dot_nt(dyd, w2).astype(BF16).astype(F32)
    dh1 = (da * h3 * sig * (1.0 + h1 * (1.0 - sig))).astype(BF16)
    dh3 = (da * silu).astype(BF16)
    return act, dh1, dh3


class Place:
    def __init__(self):
        self.me = lax.axis_index('ep')
        self.core = lax.rem(self.me, 2)
        self.chip = self.me // 2
        self.x = lax.rem(self.chip, SIDE)
        self.y = self.chip // SIDE
        self.partner = self.me + 1 - 2 * self.core

    def chip_at(self, ox, oy):
        return lax.rem(self.y + oy + SIDE, SIDE) * SIDE + lax.rem(self.x + ox + SIDE, SIDE)

    def dev(self, ox, oy):
        return self.chip_at(ox, oy) * 2 + self.core


def pick(k, values):
    out = jnp.int32(values[0])
    for j in range(1, len(values)):
        out = jnp.where(k == j, jnp.int32(values[j]), out)
    return out


class Gather:
    AXES = (((1, 0), (0, 1)), ((0, 1), (1, 0)))

    def __init__(self, place, src, out, ssem, rsem):
        self.p, self.src, self.out, self.ssem, self.rsem = place, src, out, ssem, rsem
        self.half = src.shape[0] // 2
        self.sent = []
        self.ids = {}

    def rows(self, h, q=None):
        if q is None:
            return (h * self.half, self.half)
        return (h * self.half + q * (self.half // 2), self.half // 2)

    def rid(self, *key):
        return self.ids.setdefault(key, len(self.ids))

    def send(self, origin, rows, to, rid, own=False):
        k = len(self.sent)
        cut = pl.ds(*rows)
        self.sent.append(rows[1])
        pltpu.make_async_remote_copy(
            src_ref=self.src.at[cut] if own else self.out.at[origin, cut],
            dst_ref=self.out.at[origin, cut],
            send_sem=self.ssem.at[k], recv_sem=self.rsem.at[rid],
            device_id={'ep': to}, device_id_type=MESH).start()

    def wait(self, rows, rid):
        ref = self.out.at[0, pl.ds(*rows)]
        pltpu.make_async_remote_copy(src_ref=ref, dst_ref=ref, send_sem=self.ssem.at[0], recv_sem=self.rsem.at[rid],
                                     device_id={'ep': self.p.partner}, device_id_type=MESH).wait_recv()

    def to_partner(self, ox, oy, rows, own=False):
        self.send(self.p.dev(ox, oy), rows, self.p.partner, self.rid('p', ox % SIDE, oy % SIDE, rows), own)

    def begin(self):
        for h in (0, 1):
            e1, e2 = self.AXES[h]
            for s in (1, -1):
                self.send(self.p.me, self.rows(h), self.p.dev(s * e1[0], s * e1[1]), self.rid('1', h, s), True)
            for s in (1, -1):
                self.send(self.p.me, self.rows(h), self.p.dev(s * e2[0], s * e2[1]), self.rid('2', h, s, 0), True)
        self.to_partner(0, 0, (0, 2 * self.half), True)

    def first(self, h):
        e1, e2 = self.AXES[h]
        for s in (1, -1):
            ox, oy = -s * e1[0], -s * e1[1]
            self.wait(self.rows(h), self.rid('1', h, s))
            o = self.p.dev(ox, oy)
            part = self.rows(h, 0 if s == 1 else 1)
            self.send(o, part, self.p.dev(s * e1[0], s * e1[1]), self.rid('1f', h, s))
            for t in (1, -1):
                self.send(o, self.rows(h), self.p.dev(t * e2[0], t * e2[1]), self.rid('2', h, t, -s))
            self.to_partner(ox, oy, self.rows(h))

    def second(self, h, j):
        e1, e2 = self.AXES[h]
        for s in (1, -1):
            ox, oy = j * e1[0] - s * e2[0], j * e1[1] - s * e2[1]
            part = self.rows(h, 0 if s == 1 else 1)
            if j == 2:
                for q in (0, 1):
                    self.wait(self.rows(h, q), self.rid('2', h, s, 2, q))
            else:
                self.wait(self.rows(h), self.rid('2', h, s, j))
            self.send(self.p.dev(ox, oy), part, self.p.dev(s * e2[0], s * e2[1]), self.rid('2f', h, s, j))
            self.to_partner(ox, oy, self.rows(h))

    def first_far(self, h):
        e1, e2 = self.AXES[h]
        ox, oy = 2 * e1[0], 2 * e1[1]
        for s in (1, -1):
            q = 0 if s == 1 else 1
            self.wait(self.rows(h, q), self.rid('1f', h, s))
            for t in (1, -1):
                self.send(self.p.dev(ox, oy), self.rows(h, q), self.p.dev(t * e2[0], t * e2[1]), self.rid('2', h, t, 2, q))
        self.to_partner(ox, oy, self.rows(h))

    def second_far(self, j):
        for h in (0, 1):
            e1, e2 = self.AXES[h]
            ox, oy = j * e1[0] + 2 * e2[0], j * e1[1] + 2 * e2[1]
            for s in (1, -1):
                self.wait(self.rows(h, 0 if s == 1 else 1), self.rid('2f', h, s, j))
            self.to_partner(ox, oy, self.rows(h))

    def from_partner(self, ox, oy):
        parts = [(key[3], r) for key, r in self.ids.items() if key[:3] == ('p', ox, oy)]
        assert sum(rows[1] for rows, _ in parts) == 2 * self.half
        for rows, r in parts:
            self.wait(rows, r)

    def finish(self):
        for k, size in enumerate(self.sent):
            ref = self.out.at[0, pl.ds(0, size)]
            pltpu.make_async_remote_copy(src_ref=ref, dst_ref=ref, send_sem=self.ssem.at[k], recv_sem=self.rsem.at[0],
                                         device_id={'ep': self.p.partner}, device_id_type=MESH).wait_send()


def layer_kernel(group, dy, maps, idx, yd, x, h1, h3, w1, w3, w2,
                 dx_out, dg_out, g1_out, g3_out, g2_out, everyone, staged, back,
                 maps_all, w1_v, w3_v, w2_v, dy_t, h1_t, h3_t, dx_t, yd_t, dyo, x_t, back_t, dyd_s, act_s, dh1_s, dh3_s,
                 g1, g3, g2, acc, idx_b,
                 ag_ssem, ag_rsem, m_ssem, m_rsem, r_ssem, r_rsem, own_sem, w_sem, in_sem, st_sem, yd_sem, x_sem, b_sem, g_sem):
    p = Place()
    me = p.me
    n_micro, tokens, d = dy.shape
    capacity = back.shape[2] // 2
    rows = 2 * capacity
    per_micro = rows * UNITS

    barrier = pltpu.get_barrier_semaphore()

    def greet(k, c):
        pl.semaphore_signal(barrier, inc=1, device_id={'ep': lax.rem(me + k, group)}, device_id_type=MESH)
        return c

    lax.fori_loop(1, group, greet, 0)

    weights = [pltpu.make_async_copy(a, b, w_sem.at[k]) for k, (a, b) in enumerate(((w1, w1_v), (w3, w3_v), (w2, w2_v)))]
    own = [pltpu.make_async_copy(dy.at[m], everyone.at[m, me], own_sem.at[m]) for m in range(n_micro)]
    own_maps = pltpu.make_async_copy(maps.at[me], maps_all.at[me], own_sem.at[n_micro])
    own_dy = pltpu.make_async_copy(dy, dyo, own_sem.at[n_micro + 1])
    own_dy.start()

    yd_tokens = yd_t.shape[1]
    yd_steps = yd.shape[0] // yd_tokens

    def yd_copy(i):
        slot = lax.rem(i, 2)
        return pltpu.make_async_copy(yd.at[pl.ds(i * yd_tokens, yd_tokens)], yd_t.at[slot], yd_sem.at[slot])

    yd_copy(0).start()
    pl.semaphore_wait(barrier, group - 1)

    gathers = [Gather(p, dy.at[m], everyone.at[m], ag_ssem.at[m], ag_rsem.at[m]) for m in range(n_micro)]
    gathers[0].begin()

    def map_copy(to, origin, slot_s, slot_r):
        return pltpu.make_async_remote_copy(src_ref=maps.at[to], dst_ref=maps_all.at[origin], send_sem=m_ssem.at[slot_s],
                                            recv_sem=m_rsem.at[slot_r], device_id={'ep': to}, device_id_type=MESH)

    def send_map(k, c):
        to = lax.rem(me + k, group)
        map_copy(to, me, k, me).start()
        return c

    lax.fori_loop(1, group, send_map, 0)
    own_maps.start()
    for c in own + weights:
        c.start()

    own_dy.wait()

    def gate_step(i, c):
        @pl.when(i + 1 < yd_steps)
        def _():
            yd_copy(i + 1).start()
        yd_copy(i).wait()
        slot = lax.rem(i, 2)
        per = tokens // yd_tokens
        m = i // per
        r0 = pl.multiple_of(lax.rem(i, per) * yd_tokens, yd_tokens)
        a = dyo[m, pl.ds(r0, yd_tokens), :].astype(F32)
        b = yd_t[slot].astype(F32)
        dg_out[pl.ds(pl.multiple_of(i * yd_tokens, yd_tokens), yd_tokens), :] = jnp.sum(a[:, None, :] * b, axis=-1)
        return c

    lax.fori_loop(0, yd_steps, gate_step, 0)

    def spread(m):
        for j in range(idx.shape[2]):
            idx_b[m, j] = jnp.broadcast_to(idx[m, :, j:j + 1], idx_b.shape[2:])

    for m in range(n_micro):
        spread(m)

    def unit_of(i):
        m = i // UNITS
        k = lax.rem(i, UNITS)
        u = p.chip_at(pick(k, [o[0] for o in ORDER]), pick(k, [o[1] for o in ORDER]))
        return m, k, u

    def loads(i):
        m, k, u = unit_of(i)
        slot = lax.rem(i, 2)
        r0 = pl.multiple_of(u * rows, 16)
        return [pltpu.make_async_copy(everyone.at[m, pl.ds(2 * u, 2)], dy_t.at[slot], in_sem.at[slot, 0]),
                pltpu.make_async_copy(h1.at[m, pl.ds(r0, rows)], h1_t.at[slot], in_sem.at[slot, 1]),
                pltpu.make_async_copy(h3.at[m, pl.ds(r0, rows)], h3_t.at[slot], in_sem.at[slot, 2])]

    def stage_copy(i):
        m, k, u = unit_of(i)
        slot = lax.rem(i, 2)
        return pltpu.make_async_copy(dx_t.at[slot], staged.at[m, u], st_sem.at[slot])

    def return_copy(i, w, to, u, m):
        cut = pl.ds(pl.multiple_of(w * capacity, 8), capacity)
        mine = pl.ds(pl.multiple_of(p.core * capacity, 8), capacity)
        return pltpu.make_async_remote_copy(src_ref=staged.at[m, u, cut], dst_ref=back.at[m, p.chip, mine],
                                            send_sem=r_ssem.at[i * 2 + w], recv_sem=r_rsem.at[m * group + me],
                                            device_id={'ep': to}, device_id_type=MESH)

    def own_return(m):
        mine = pl.ds(pl.multiple_of(p.core * capacity, 8), capacity)
        return pltpu.make_async_copy(staged.at[m, p.chip, mine], back.at[m, p.chip, mine], own_sem.at[n_micro + 2 + m])

    def send_back(i):
        m, k, u = unit_of(i)

        @pl.when(k == 0)
        def _():
            return_copy(i, 1 - p.core, p.partner, u, m).start()
            own_return(m).start()

        @pl.when(k > 0)
        def _():
            for w in (0, 1):
                return_copy(i, w, 2 * u + w, u, m).start()

    a, b = gathers
    events = {i: [] for i in range(-1, n_micro * UNITS)}
    events[-1] += [lambda: a.first(0), lambda: a.first(1), lambda: a.second(0, 0), lambda: a.second(1, 0), b.begin]
    events[0] += [lambda: a.first_far(0), lambda: a.first_far(1)]
    events[1] += [lambda: a.second(0, 1), lambda: a.second(1, 1)]
    events[2] += [lambda: a.second(0, -1), lambda: a.second(1, -1)]
    events[4] += [lambda: a.second(0, 2), lambda: a.second(1, 2)]
    events[5] += [lambda: b.first(0), lambda: b.first(1)]
    events[6] += [lambda: b.second(0, 0), lambda: b.second(1, 0)]
    events[8] += [lambda: a.second_far(0)]
    events[9] += [lambda: b.first_far(0), lambda: b.first_far(1)]
    events[10] += [lambda: a.second_far(1), lambda: a.second_far(-1), lambda: a.second_far(2)]
    events[11] += [lambda: b.second(0, 1), lambda: b.second(1, 1)]
    events[12] += [lambda: b.second(0, -1), lambda: b.second(1, -1)]
    events[14] += [lambda: b.second(0, 2), lambda: b.second(1, 2)]
    events[UNITS + 8] += [lambda: b.second_far(0)]
    events[UNITS + 10] += [lambda: b.second_far(1), lambda: b.second_far(-1), lambda: b.second_far(2)]
    for m, g in enumerate(gathers):
        for k, (ox, oy) in enumerate(ORDER):
            events[m * UNITS + k - 1].append(functools.partial(g.from_partner, ox, oy))
        events[m * UNITS - 1].append(own[m].wait)

    for e in events[-1]:
        e()

    def recv_map(k, c):
        s = lax.rem(me + k, group)
        map_copy(s, s, k, s).wait()
        return c

    lax.fori_loop(1, group, recv_map, 0)
    own_maps.wait()
    for c in loads(0):
        c.start()
    for c in weights:
        c.wait()

    total = n_micro * UNITS

    def unit_step(i, c):
        for k in range(total):
            if events[k]:
                @pl.when(i == k)
                def _():
                    for e in events[k]:
                        e()

        @pl.when(i + 1 < total)
        def _():
            for t in loads(i + 1):
                t.start()

        @pl.when(i >= 1)
        def _():
            stage_copy(i - 1).wait()
            send_back(i - 1)

        for t in loads(i):
            t.wait()
        m, k, u = unit_of(i)
        slot = lax.rem(i, 2)
        pos = jnp.concatenate([maps_all[2 * u, 2 * m], maps_all[2 * u + 1, 2 * m]], axis=1)
        gate = jnp.concatenate([maps_all[2 * u, 2 * m + 1], maps_all[2 * u + 1, 2 * m + 1]], axis=1)
        dyd = gather_rows(pos, gate, dy_t[slot].reshape(2 * tokens, d), rows)
        act, dh1, dh3 = swiglu_grads(dyd, h1_t[slot], h3_t[slot], w2_v[...])
        dx_t[slot] = (dot_nt(dh1, w1_v[...]) + dot_nt(dh3, w3_v[...])).astype(BF16)
        stage_copy(i).start()
        at = pl.ds(pl.multiple_of(m * per_micro + u * rows, 16), rows)
        dyd_s[at, :] = dyd
        act_s[at, :] = act
        dh1_s[at, :] = dh1
        dh3_s[at, :] = dh3
        return c

    lax.fori_loop(0, total, unit_step, 0)
    stage_copy(total - 1).wait()
    send_back(total - 1)

    depth = x_t.shape[1]
    x_steps = n_micro * per_micro // depth

    def x_copy(i):
        slot = lax.rem(i, 2)
        return pltpu.make_async_copy(x.at[pl.ds(pl.multiple_of(i * depth, depth), depth)], x_t.at[slot], x_sem.at[slot])

    x_copy(0).start()
    for g in (g1, g3, g2):
        g[...] = jnp.zeros_like(g)

    def weight_step(i, c):
        @pl.when(i + 1 < x_steps)
        def _():
            x_copy(i + 1).start()
        x_copy(i).wait()
        at = pl.ds(pl.multiple_of(i * depth, depth), depth)
        xt = x_t[lax.rem(i, 2)]
        g1[...] += dot_tn(xt, dh1_s[at, :])
        g3[...] += dot_tn(xt, dh3_s[at, :])
        g2[...] += dot_tn(act_s[at, :], dyd_s[at, :])
        return c

    lax.fori_loop(0, x_steps, weight_step, 0)
    outs = [pltpu.make_async_copy(s, t, g_sem.at[k]) for k, (s, t) in enumerate(((g1, g1_out), (g3, g3_out), (g2, g2_out)))]
    for c in outs:
        c.start()

    def arrive(i):
        m, k, u = unit_of(i)

        def wait_from(s):
            cut = pl.ds(0, capacity)
            pltpu.make_async_remote_copy(src_ref=back.at[m, u, cut], dst_ref=back.at[m, u, cut], send_sem=r_ssem.at[0],
                                         recv_sem=r_rsem.at[m * group + s], device_id={'ep': p.partner}, device_id_type=MESH).wait_recv()

        @pl.when(k == 0)
        def _():
            wait_from(p.partner)
            own_return(m).wait()

        @pl.when(k > 0)
        def _():
            wait_from(2 * u)
            wait_from(2 * u + 1)

    def back_copy(i):
        m, k, u = unit_of(i)
        slot = lax.rem(i, 2)
        return pltpu.make_async_copy(back.at[m, u], back_t.at[slot], b_sem.at[slot])

    arrive(0)
    back_copy(0).start()

    def combine_step(i, c):
        @pl.when(i + 1 < total)
        def _():
            arrive(i + 1)
            back_copy(i + 1).start()
        back_copy(i).wait()
        m, k, u = unit_of(i)
        lanes = idx_b.shape[3]
        base = u * rows
        hits = []
        for c0 in range(0, rows, lanes):
            want = lax.broadcasted_iota(jnp.int32, (tokens, lanes), 1) + (base + c0)
            hit = idx_b[m, 0] == want
            for j in range(1, idx_b.shape[1]):
                hit = hit | (idx_b[m, j] == want)
            hits.append(jnp.where(hit, 1.0, 0.0))
        sel = jnp.concatenate(hits, axis=1)[:, :rows].astype(BF16)
        part = dot_nn(sel, back_t[lax.rem(i, 2)])

        @pl.when(k == 0)
        def _():
            acc[...] = part

        @pl.when(k > 0)
        def _():
            acc[...] += part

        @pl.when(k == UNITS - 1)
        def _():
            dx_out[m] = acc[...].astype(BF16)
        return c

    lax.fori_loop(0, total, combine_step, 0)

    for g in gathers:
        g.finish()

    def sent(i, c):
        m, k, u = unit_of(i)

        @pl.when(k == 0)
        def _():
            return_copy(i, 1 - p.core, p.partner, u, m).wait_send()

        @pl.when(k > 0)
        def _():
            for w in (0, 1):
                return_copy(i, w, 2 * u + w, u, m).wait_send()
        return c

    lax.fori_loop(0, total, sent, 0)
    for c in outs:
        c.wait()


def layer_call(group, dy, maps, idx, yd, x, h1, h3, w1, w3, w2):
    n_micro, tokens, d = dy.shape
    f = h1.shape[2]
    rows = h1.shape[1] // UNITS
    saved = n_micro * h1.shape[1]
    hbm = pl.BlockSpec(memory_space=pltpu.HBM)
    vmem = pl.BlockSpec(memory_space=pltpu.VMEM)
    dma = pltpu.SemaphoreType.DMA
    out = pl.pallas_call(
        functools.partial(layer_kernel, group),
        in_specs=[hbm, hbm, vmem, hbm, hbm, hbm, hbm, hbm, hbm, hbm],
        out_specs=[vmem, vmem, hbm, hbm, hbm, hbm, hbm, hbm],
        out_shape=[jax.ShapeDtypeStruct((n_micro, tokens, d), BF16),
                   jax.ShapeDtypeStruct((n_micro * tokens, yd.shape[1]), F32),
                   jax.ShapeDtypeStruct((d, f), F32), jax.ShapeDtypeStruct((d, f), F32), jax.ShapeDtypeStruct((f, d), F32),
                   jax.ShapeDtypeStruct((n_micro, group, tokens, d), BF16),
                   jax.ShapeDtypeStruct((n_micro, UNITS, rows, d), BF16),
                   jax.ShapeDtypeStruct((n_micro, UNITS, rows, d), BF16)],
        scratch_shapes=[pltpu.VMEM(maps.shape, F32),
                        pltpu.VMEM((d, f), BF16), pltpu.VMEM((d, f), BF16), pltpu.VMEM((f, d), BF16),
                        pltpu.VMEM((2, 2, tokens, d), BF16), pltpu.VMEM((2, rows, f), BF16), pltpu.VMEM((2, rows, f), BF16),
                        pltpu.VMEM((2, rows, d), BF16), pltpu.VMEM((2, 32) + yd.shape[1:], BF16), pltpu.VMEM(dy.shape, BF16),
                        pltpu.VMEM((2, 256, d), BF16), pltpu.VMEM((2, rows, d), BF16),
                        pltpu.VMEM((saved, d), BF16), pltpu.VMEM((saved, f), BF16), pltpu.VMEM((saved, f), BF16), pltpu.VMEM((saved, f), BF16),
                        pltpu.VMEM((d, f), F32), pltpu.VMEM((d, f), F32), pltpu.VMEM((f, d), F32),
                        pltpu.VMEM((tokens, d), F32), pltpu.VMEM((n_micro, idx.shape[2], tokens, 128), jnp.int32),
                        dma((n_micro, 80)), dma((n_micro, 80)), dma((group,)), dma((group,)),
                        dma((2 * n_micro * UNITS,)), dma((n_micro * group,)), dma((n_micro + 2 + n_micro,)), dma((3,)),
                        dma((2, 3)), dma((2,)), dma((2,)), dma((2,)), dma((2,)), dma((3,))],
        compiler_params=pltpu.CompilerParams(collective_id=0, has_side_effects=True, vmem_limit_bytes=64 * 2**20 - 2**17),
        name='layer')(dy, maps, idx, yd, x, h1, h3, w1, w3, w2)
    return out[:5]


def solution(mesh):
    group = mesh.shape['ep']
    tok_spec = P(None, ('dp', 'ep'))
    w_spec = P('ep')
    grad_w_spec = P(('dp', 'ep'))

    def local_step(grad_out, expert_out, gate_vals, topk_idx, slot_idx, x_dispatch, h1_pre, h3_pre, w_gate, w_up, w_down):
        n_micro, tokens, top_k, d = expert_out.shape
        experts = group * w_gate.shape[0]
        capacity = x_dispatch.shape[2] // group
        me = lax.axis_index('ep')
        idx_t = jnp.swapaxes(topk_idx, 1, 2)[:, :, None, :]
        slot_t = jnp.swapaxes(slot_idx, 1, 2)[:, :, None, :]
        gate_t = jnp.swapaxes(gate_vals, 1, 2)[:, :, None, :]
        match = idx_t == jnp.arange(experts, dtype=jnp.int32)[None, None, :, None]
        slot_map = jnp.max(jnp.where(match, slot_t, -1), axis=1)
        pos_map = jnp.where(slot_map >= 0, slot_map + capacity * lax.rem(me, 2), -1).astype(F32)
        gate_map = jnp.sum(jnp.where(match, gate_t, 0.0), axis=1)
        maps = jnp.stack([pos_map, gate_map], axis=1)
        maps = jnp.moveaxis(maps, 2, 0).reshape(experts, 2 * n_micro, 1, tokens)
        send_rows = jnp.where(slot_idx >= 0, topk_idx * capacity + slot_idx, -1)
        dx, dg, g1, g3, g2 = layer_call(
            group, grad_out, maps, send_rows, expert_out.reshape(n_micro * tokens, top_k, d),
            x_dispatch.reshape(-1, d), h1_pre[:, 0], h3_pre[:, 0], w_gate[0], w_up[0], w_down[0])
        return dx, dg.reshape(n_micro, tokens, top_k), g1[None], g3[None], g2[None]

    in_specs = (tok_spec, tok_spec, tok_spec, tok_spec, tok_spec, tok_spec, tok_spec, tok_spec, w_spec, w_spec, w_spec)
    out_specs = (tok_spec, tok_spec, grad_w_spec, grad_w_spec, grad_w_spec)
    return jax.shard_map(local_step, mesh=mesh, in_specs=in_specs, out_specs=out_specs, check_vma=False)
```

time: 595 us -> 285 us (0.48)
  the two profiles are of different devices: /device:TPU:103 before, /device:TPU:105 now
where the time goes in v2:
time: 285 us; the launch traced here: 283 us
  Pallas kernels  266 us (93%)
  local copies, waits for them, and re-layouts  12 us (4%)
  other arithmetic  3.82 us (1%)
    pallas_call x1, Pallas kernels, layer_call(): pl.pallas_call(functools.partial(layer_kernel, group), in_specs=[hbm, hbm...  266 us
    unnamed x10, local copies, waits for them, and re-layouts  10.8 us

profile of v2, /device:TPU:105, one launch (start us, length us, event | category | flops | bytes accessed | tf_op | source)
XLA Modules:
  0.0 282.9 jit_solution(9394592370453934468)
XLA Ops:
  0.6 0.7 broadcast_compare_fusion
  1.4 0.7 broadcast_multiply_fusion
  2.1 0.2 copy.32
  2.3 0.8 select_reduce_fusion
  3.1 0.8 select_reduce_fusion.1
  3.9 0.1 copy.29
  4.0 0.9 reshape.48.maps
  4.9 0.1 copy.30
  5.0 0.8 copy.31
  5.9 0.7 add_select_fusion.idx
  6.6 266.4 %layer.1 = (bf16[2,256,1024]{2,1,0:T(8,128)(2,1)}, f32[512,8]{1,0:T(8,128)}, f32[1024,512]{1,0:T(8,128)}, f32[1024,512]{1,0:T(8,128)}, f32[512,1024]{1,0:T(8,128...) custom-call(bf16[2,256,1024]{2,1,0:T(8,128)(2,1)} %dy.1, ...), custom_call_target="tpu_custom_call" | custom-call | tf_op jit(solution)/shard_map/layer/pallas_call | solution.py:488
  273.0 0.0 copy-start
  273.0 1.8 copy.33
  274.8 0.0 copy-start.1
  274.8 2.4 copy.38
  277.2 3.1 %copy.39 = f32[1,1024,512]{2,1,0:T(8,128)} copy(f32[1,1024,512]{2,1,0:T(8,128)} %bitcast.25) | data formatting | bytes 4194304
  280.3 0.0 copy-done.1
  280.3 1.3 copy.40
  281.6 0.0 copy-done
  281.6 1.3 copy.41
  (2 shorter events, 0.0 us)
Async XLA Ops:
  273.0 8.6 %copy-start = (f32[512,1024]{1,0:T(8,128)S(1)}, f32[512,1024]{1,0:T(8,128)}, u32[]{:S(2)}) copy-start(f32[512,1024]{1,0:T(8,128)} %get-tuple-element.14) | copy-start | bytes 6291460
  274.8 5.5 %copy-start.1 = (f32[1024,512]{1,0:T(8,128)S(1)}, f32[1024,512]{1,0:T(8,128)}, u32[]{:S(2)}) copy-start(f32[1024,512]{1,0:T(8,128)} %get-tuple-element.13) | copy-start | bytes 6291460

commit v3 on v2

v3 whole, which is shorter than its diff:
```python
import functools
import jax
import jax.numpy as jnp
from jax import lax
from jax.experimental import pallas as pl
from jax.experimental.pallas import tpu as pltpu
from jax.sharding import PartitionSpec as P

F32 = jnp.float32
BF16 = jnp.bfloat16
MESH = pl.DeviceIdType.MESH
SIDE = 4
ORDER = ((0, 0), (1, 0), (3, 0), (0, 1), (0, 3), (1, 1), (3, 3), (1, 3), (3, 1), (2, 0), (0, 2), (2, 1), (1, 2), (2, 3), (3, 2), (2, 2))
UNITS = len(ORDER)
FAR_FIRST = ((0, 2), (1, 2), (3, 2), (2, 2), (2, 0), (2, 1), (2, 3), (0, 1), (1, 1), (3, 1), (1, 0), (1, 3), (0, 3), (3, 3), (3, 0), (0, 0))
PART_ORDER = (2, 1, 3, 0)


def dot_nn(a, b):
    return lax.dot_general(a, b, (((1,), (0,)), ((), ())), preferred_element_type=F32)


def dot_nt(a, b):
    return lax.dot_general(a, b, (((1,), (1,)), ((), ())), preferred_element_type=F32)


def dot_tn(a, b):
    return lax.dot_general(a, b, (((0,), (0,)), ((), ())), preferred_element_type=F32)


def gather_rows(pos, gate, dy, rows):
    tokens = pos.shape[1]
    hit = lax.broadcasted_iota(jnp.int32, (rows, tokens), 0).astype(F32) == pos
    gate_col = jnp.sum(jnp.where(hit, gate, 0.0), axis=1, keepdims=True)
    onehot = jnp.where(hit, 1.0, 0.0).astype(BF16)
    return (dot_nn(onehot, dy) * gate_col).astype(BF16)


def swiglu_grads(dyd, h1, h3, w2):
    h1 = h1.astype(F32)
    h3 = h3.astype(F32)
    sig = jax.nn.sigmoid(h1)
    silu = h1 * sig
    act = (silu * h3).astype(BF16)
    da = dot_nt(dyd, w2).astype(BF16).astype(F32)
    dh1 = (da * h3 * sig * (1.0 + h1 * (1.0 - sig))).astype(BF16)
    dh3 = (da * silu).astype(BF16)
    return act, dh1, dh3


class Place:
    def __init__(self):
        self.me = lax.axis_index('ep')
        self.core = lax.rem(self.me, 2)
        self.chip = self.me // 2
        self.x = lax.rem(self.chip, SIDE)
        self.y = self.chip // SIDE
        self.partner = self.me + 1 - 2 * self.core

    def chip_at(self, ox, oy):
        return lax.rem(self.y + oy + SIDE, SIDE) * SIDE + lax.rem(self.x + ox + SIDE, SIDE)

    def dev(self, ox, oy):
        return self.chip_at(ox, oy) * 2 + self.core


def pick(k, values):
    out = jnp.int32(values[0])
    for j in range(1, len(values)):
        out = jnp.where(k == j, jnp.int32(values[j]), out)
    return out


class Gather:
    AXES = (((1, 0), (0, 1)), ((0, 1), (1, 0)))

    def __init__(self, place, src, out, ssem, rsem):
        self.p, self.src, self.out, self.ssem, self.rsem = place, src, out, ssem, rsem
        self.half = src.shape[0] // 2
        self.sent = []
        self.ids = {}

    def rows(self, h, q=None):
        if q is None:
            return (h * self.half, self.half)
        return (h * self.half + q * (self.half // 2), self.half // 2)

    def rid(self, *key):
        return self.ids.setdefault(key, len(self.ids))

    def send(self, origin, rows, to, rid, own=False):
        k = len(self.sent)
        cut = pl.ds(*rows)
        self.sent.append(rows[1])
        pltpu.make_async_remote_copy(
            src_ref=self.src.at[cut] if own else self.out.at[origin, cut],
            dst_ref=self.out.at[origin, cut],
            send_sem=self.ssem.at[k], recv_sem=self.rsem.at[rid],
            device_id={'ep': to}, device_id_type=MESH).start()

    def wait(self, rows, rid):
        ref = self.out.at[0, pl.ds(*rows)]
        pltpu.make_async_remote_copy(src_ref=ref, dst_ref=ref, send_sem=self.ssem.at[0], recv_sem=self.rsem.at[rid],
                                     device_id={'ep': self.p.partner}, device_id_type=MESH).wait_recv()

    def to_partner(self, ox, oy, rows, own=False):
        self.send(self.p.dev(ox, oy), rows, self.p.partner, self.rid('p', ox % SIDE, oy % SIDE, rows), own)

    def begin(self):
        for h in (0, 1):
            e1, e2 = self.AXES[h]
            for s in (1, -1):
                self.send(self.p.me, self.rows(h), self.p.dev(s * e1[0], s * e1[1]), self.rid('1', h, s), True)
            for s in (1, -1):
                self.send(self.p.me, self.rows(h), self.p.dev(s * e2[0], s * e2[1]), self.rid('2', h, s, 0), True)
        self.to_partner(0, 0, (0, 2 * self.half), True)

    def first(self, h):
        e1, e2 = self.AXES[h]
        for s in (1, -1):
            ox, oy = -s * e1[0], -s * e1[1]
            self.wait(self.rows(h), self.rid('1', h, s))
            o = self.p.dev(ox, oy)
            part = self.rows(h, 0 if s == 1 else 1)
            self.send(o, part, self.p.dev(s * e1[0], s * e1[1]), self.rid('1f', h, s))
            for t in (1, -1):
                self.send(o, self.rows(h), self.p.dev(t * e2[0], t * e2[1]), self.rid('2', h, t, -s))
            self.to_partner(ox, oy, self.rows(h))

    def second(self, h, j):
        e1, e2 = self.AXES[h]
        for s in (1, -1):
            ox, oy = j * e1[0] - s * e2[0], j * e1[1] - s * e2[1]
            part = self.rows(h, 0 if s == 1 else 1)
            if j == 2:
                for q in (0, 1):
                    self.wait(self.rows(h, q), self.rid('2', h, s, 2, q))
            else:
                self.wait(self.rows(h), self.rid('2', h, s, j))
            self.send(self.p.dev(ox, oy), part, self.p.dev(s * e2[0], s * e2[1]), self.rid('2f', h, s, j))
            self.to_partner(ox, oy, self.rows(h))

    def first_far(self, h):
        e1, e2 = self.AXES[h]
        ox, oy = 2 * e1[0], 2 * e1[1]
        for s in (1, -1):
            q = 0 if s == 1 else 1
            self.wait(self.rows(h, q), self.rid('1f', h, s))
            for t in (1, -1):
                self.send(self.p.dev(ox, oy), self.rows(h, q), self.p.dev(t * e2[0], t * e2[1]), self.rid('2', h, t, 2, q))
        self.to_partner(ox, oy, self.rows(h))

    def second_far(self, j):
        for h in (0, 1):
            e1, e2 = self.AXES[h]
            ox, oy = j * e1[0] + 2 * e2[0], j * e1[1] + 2 * e2[1]
            for s in (1, -1):
                self.wait(self.rows(h, 0 if s == 1 else 1), self.rid('2f', h, s, j))
            self.to_partner(ox, oy, self.rows(h))

    def from_partner(self, ox, oy):
        parts = [(key[3], r) for key, r in self.ids.items() if key[:3] == ('p', ox, oy)]
        assert sum(rows[1] for rows, _ in parts) == 2 * self.half
        for rows, r in parts:
            self.wait(rows, r)

    def finish(self):
        for k, size in enumerate(self.sent):
            ref = self.out.at[0, pl.ds(0, size)]
            pltpu.make_async_remote_copy(src_ref=ref, dst_ref=ref, send_sem=self.ssem.at[k], recv_sem=self.rsem.at[0],
                                         device_id={'ep': self.p.partner}, device_id_type=MESH).wait_send()


def layer_kernel(group, dy, topk, slots, gates, yd, x, h1, h3, w1, w3, w2,
                 dx_out, dg_out, g1_out, g3_out, g2_out, everyone, staged, lined, parts,
                 maps, maps_all, idx_all, w1_v, w3_v, w2_v, dy_t, h1_t, h3_t, dx_t, yd_t, dyo, x_t, line_t, sum_s, part_t,
                 dyd_s, act_s, dh1_s, dh3_s, g1, g3, g2,
                 ag_ssem, ag_rsem, m_ssem, m_rsem, i_ssem, i_rsem, r_ssem, r_rsem, p_ssem, p_rsem,
                 own_sem, w_sem, in_sem, st_sem, yd_sem, x_sem, l_sem, f_sem, g_sem):
    p = Place()
    me = p.me
    n_micro, tokens, d = dy.shape
    top_k = topk.shape[1]
    rows = lined.shape[4]
    capacity = rows // 2
    wide = d // 2
    per_micro = rows * UNITS

    barrier = pltpu.get_barrier_semaphore()

    def greet(k, c):
        pl.semaphore_signal(barrier, inc=1, device_id={'ep': lax.rem(me + k, group)}, device_id_type=MESH)
        return c

    lax.fori_loop(1, group, greet, 0)

    weights = [pltpu.make_async_copy(a, b, w_sem.at[k]) for k, (a, b) in enumerate(((w1, w1_v), (w3, w3_v), (w2, w2_v)))]
    own = [pltpu.make_async_copy(dy.at[m], everyone.at[m, me], own_sem.at[m]) for m in range(n_micro)]
    own_dy = pltpu.make_async_copy(dy, dyo, own_sem.at[n_micro])
    own_dy.start()
    yd_tokens = yd_t.shape[1]
    yd_steps = yd.shape[0] // yd_tokens

    def yd_copy(i):
        slot = lax.rem(i, 2)
        return pltpu.make_async_copy(yd.at[pl.ds(i * yd_tokens, yd_tokens)], yd_t.at[slot], yd_sem.at[slot])

    yd_copy(0).start()

    for m in range(n_micro):
        experts = lax.broadcasted_iota(jnp.int32, (group, tokens), 0)
        pos = jnp.full((group, tokens), -1, jnp.int32)
        gate = jnp.zeros((group, tokens), F32)
        for j in range(top_k):
            same = experts == topk[m, j:j + 1, :]
            at = slots[m, j:j + 1, :]
            pos = jnp.where(same, jnp.where(at >= 0, at + p.core * capacity, -1), pos)
            gate = jnp.where(same, gates[m, j:j + 1, :], gate)
        pos = pos.astype(F32)
        for e in range(group):
            maps[e, 2 * m] = pos[e:e + 1, :]
            maps[e, 2 * m + 1] = gate[e:e + 1, :]
        mine = jnp.where(slots[m] >= 0, topk[m] * capacity + slots[m], -1)
        idx_all[p.y, m] = mine
        idx_all[SIDE + p.x, m] = mine
    maps_all[me] = maps[me]

    pl.semaphore_wait(barrier, group - 1)

    gathers = [Gather(p, dy.at[m], everyone.at[m], ag_ssem.at[m], ag_rsem.at[m]) for m in range(n_micro)]
    gathers[0].begin()

    def map_copy(to, origin, slot_s, slot_r):
        return pltpu.make_async_remote_copy(src_ref=maps.at[to], dst_ref=maps_all.at[origin], send_sem=m_ssem.at[slot_s],
                                            recv_sem=m_rsem.at[slot_r], device_id={'ep': to}, device_id_type=MESH)

    def send_map(k, c):
        to = lax.rem(me + k, group)
        map_copy(to, me, k, me).start()
        return c

    lax.fori_loop(1, group, send_map, 0)

    def idx_copy(half, o):
        at = p.y if half == 0 else SIDE + p.x
        to = p.dev(0, o) if half == 0 else p.dev(o, 0)
        return pltpu.make_async_remote_copy(src_ref=idx_all.at[at], dst_ref=idx_all.at[at], send_sem=i_ssem.at[half * SIDE + o],
                                            recv_sem=i_rsem.at[at], device_id={'ep': to}, device_id_type=MESH)

    def idx_wait(half, o):
        at = lax.rem(p.y + o, SIDE) if half == 0 else SIDE + lax.rem(p.x + o, SIDE)
        pltpu.make_async_remote_copy(src_ref=idx_all.at[at], dst_ref=idx_all.at[at], send_sem=i_ssem.at[0], recv_sem=i_rsem.at[at],
                                     device_id={'ep': p.partner}, device_id_type=MESH).wait_recv()

    for half in (0, 1):
        for o in range(1, SIDE):
            idx_copy(half, o).start()
    for c in own + weights:
        c.start()

    own_dy.wait()

    def gate_step(i, c):
        @pl.when(i + 1 < yd_steps)
        def _():
            yd_copy(i + 1).start()
        yd_copy(i).wait()
        slot = lax.rem(i, 2)
        per = tokens // yd_tokens
        m = i // per
        at = pl.ds(pl.multiple_of(lax.rem(i, per) * yd_tokens, yd_tokens), yd_tokens)
        fine = 32
        out = []
        for r0 in range(0, yd_tokens, fine):
            a = dyo[m, pl.ds(pl.multiple_of(lax.rem(i, per) * yd_tokens + r0, fine), fine), :].astype(F32)
            b = yd_t[slot, r0:r0 + fine].astype(F32)
            out.append(jnp.sum(a[:, None, :] * b, axis=-1))
        dg_out[m, :, at] = jnp.concatenate(out, axis=0).T
        return c

    lax.fori_loop(0, yd_steps, gate_step, 0)

    def chip_of(order, i):
        ox, oy = pick(i, [o[0] for o in order]), pick(i, [o[1] for o in order])
        return lax.rem(p.x + ox, SIDE), lax.rem(p.y + oy, SIDE)

    class Units:
        def __init__(self, m, order):
            self.m, self.order = m, order

        def loads(self, i):
            cx, cy = chip_of(self.order, i)
            u = cy * SIDE + cx
            slot = lax.rem(i, 2)
            cut = pl.ds(pl.multiple_of(u * rows, 16), rows)
            return [pltpu.make_async_copy(everyone.at[self.m, pl.ds(2 * u, 2)], dy_t.at[slot], in_sem.at[slot, 0]),
                    pltpu.make_async_copy(h1.at[self.m, cut], h1_t.at[slot], in_sem.at[slot, 1]),
                    pltpu.make_async_copy(h3.at[self.m, cut], h3_t.at[slot], in_sem.at[slot, 2])]

        def stage(self, i):
            cx, cy = chip_of(self.order, i)
            slot = lax.rem(i, 2)
            return pltpu.make_async_copy(dx_t.at[slot], staged.at[self.m, cy * SIDE + cx], st_sem.at[slot])

        def refs(self, i, half, w):
            cx, cy = chip_of(self.order, i)
            src = staged.at[self.m, cy * SIDE + cx, pl.ds(pl.multiple_of(w * capacity, 8), capacity), pl.ds(half * wide, wide)]
            mine = pl.ds(pl.multiple_of(p.core * capacity, 8), capacity)
            place = cy if half == 0 else cx
            came = p.x if half == 0 else p.y
            dst = lined.at[self.m, half, place, came, mine]
            sem = r_rsem.at[self.m, half, place, came * 2 + p.core]
            chip = p.y * SIDE + cx if half == 0 else cy * SIDE + p.x
            here = (cx == p.x) if half == 0 else (cy == p.y)
            return src, dst, sem, chip * 2 + w, here

        def each(self, i, act):
            for half in (0, 1):
                for w in (0, 1):
                    src, dst, sem, to, here = self.refs(i, half, w)
                    remote = pltpu.make_async_remote_copy(src_ref=src, dst_ref=dst, send_sem=r_ssem.at[self.m, i * 4 + half * 2 + w], recv_sem=sem,
                                                          device_id={'ep': to}, device_id_type=MESH)
                    self_too = jnp.logical_and(here, p.core == w)

                    @pl.when(jnp.logical_not(self_too))
                    def _():
                        act(remote)

                    if act is START:
                        @pl.when(self_too)
                        def _():
                            pltpu.make_async_copy(src, dst, sem).start()

        def run(self, events):
            for t in self.loads(0):
                t.start()

            def step(i, c):
                for k in range(UNITS):
                    if events.get(k):
                        @pl.when(i == k)
                        def _():
                            for e in events[k]:
                                e()

                @pl.when(i + 1 < UNITS)
                def _():
                    for t in self.loads(i + 1):
                        t.start()

                @pl.when(i >= 1)
                def _():
                    self.stage(i - 1).wait()
                    self.each(i - 1, START)

                for t in self.loads(i):
                    t.wait()
                m = self.m
                cx, cy = chip_of(self.order, i)
                u = cy * SIDE + cx
                slot = lax.rem(i, 2)
                pos = jnp.concatenate([maps_all[2 * u, 2 * m], maps_all[2 * u + 1, 2 * m]], axis=1)
                gate = jnp.concatenate([maps_all[2 * u, 2 * m + 1], maps_all[2 * u + 1, 2 * m + 1]], axis=1)
                dyd = gather_rows(pos, gate, dy_t[slot].reshape(2 * tokens, d), rows)
                act, dh1, dh3 = swiglu_grads(dyd, h1_t[slot], h3_t[slot], w2_v[...])
                dx_t[slot] = (dot_nt(dh1, w1_v[...]) + dot_nt(dh3, w3_v[...])).astype(BF16)
                self.stage(i).start()
                at = pl.ds(pl.multiple_of(u * rows, 16), rows)
                dyd_s[at, :] = dyd
                act_s[at, :] = act
                dh1_s[at, :] = dh1
                dh3_s[at, :] = dh3
                return c

            lax.fori_loop(0, UNITS, step, 0)
            self.stage(UNITS - 1).wait()
            self.each(UNITS - 1, START)

        def finish(self):
            def step(i, c):
                self.each(i, WAIT_SEND)
                return c
            lax.fori_loop(0, UNITS, step, 0)

    depth = x_t.shape[1]
    x_steps = per_micro // depth

    def weight_grads(m, events):
        def x_copy(i):
            slot = lax.rem(i, 2)
            return pltpu.make_async_copy(x.at[m, pl.ds(pl.multiple_of(i * depth, depth), depth)], x_t.at[slot], x_sem.at[slot])

        x_copy(0).start()

        def step(i, c):
            for k in range(x_steps):
                if events.get(k):
                    @pl.when(i == k)
                    def _():
                        for e in events[k]:
                            e()

            @pl.when(i + 1 < x_steps)
            def _():
                x_copy(i + 1).start()
            x_copy(i).wait()
            at = pl.ds(pl.multiple_of(i * depth, depth), depth)
            xt = x_t[lax.rem(i, 2)]
            g1[...] += dot_tn(xt, dh1_s[at, :])
            g3[...] += dot_tn(xt, dh3_s[at, :])
            g2[...] += dot_tn(act_s[at, :], dyd_s[at, :])
            return c

        lax.fori_loop(0, x_steps, step, 0)

    class Sums:
        STEPS = 2 * SIDE

        def __init__(self, m):
            self.m = m

        def where(self, i):
            half = lax.rem(i, 2)
            off = pick(i // 2, PART_ORDER)
            place = jnp.where(half == 0, lax.rem(p.y + off, SIDE), lax.rem(p.x + off, SIDE))
            return half, off, place

        def arrive(self, i):
            half, off, place = self.where(i)
            for s in range(SIDE):
                for w in (0, 1):
                    ref = lined.at[self.m, half, place, s, pl.ds(w * capacity, capacity)]
                    pltpu.make_async_remote_copy(src_ref=ref, dst_ref=ref, send_sem=r_ssem.at[0, 0], recv_sem=r_rsem.at[self.m, half, place, s * 2 + w],
                                                 device_id={'ep': p.partner}, device_id_type=MESH).wait_recv()

        def load(self, i):
            half, off, place = self.where(i)
            slot = lax.rem(i, 2)
            return pltpu.make_async_copy(lined.at[self.m, half, place], line_t.at[slot], l_sem.at[slot])

        def copy(self, i):
            half, off, place = self.where(i)
            chip = jnp.where(half == 0, place * SIDE + p.x, p.y * SIDE + place)
            mine = jnp.where(half == 0, p.y, p.x)
            return pltpu.make_async_remote_copy(src_ref=sum_s.at[self.m, i], dst_ref=parts.at[self.m, half, mine], send_sem=p_ssem.at[self.m, i],
                                                recv_sem=p_rsem.at[self.m, half, mine], device_id={'ep': chip * 2 + p.core}, device_id_type=MESH)

        def run(self):
            last = self.STEPS - 2
            self.arrive(0)
            self.load(0).start()

            def step(i, c):
                @pl.when(i + 1 < self.STEPS)
                def _():
                    self.arrive(i + 1)
                    self.load(i + 1).start()
                self.load(i).wait()

                @pl.when(jnp.logical_and(i >= 1, i <= last))
                def _():
                    self.copy(i - 1).start()

                half, off, place = self.where(i)
                home = jnp.where(half == 0, place, SIDE + place)
                slot = lax.rem(i, 2)
                total = None
                for s in range(SIDE):
                    chip = jnp.where(half == 0, p.y * SIDE + s, s * SIDE + p.x)
                    want = lax.broadcasted_iota(jnp.int32, (rows, tokens), 0) + chip * rows
                    hit = idx_all[home, self.m, 0:1, :] == want
                    for j in range(1, top_k):
                        hit = hit | (idx_all[home, self.m, j:j + 1, :] == want)
                    part = dot_tn(jnp.where(hit, 1.0, 0.0).astype(BF16), line_t[slot, s])
                    total = part if total is None else total + part
                sum_s[self.m, i] = total
                return c

            lax.fori_loop(0, self.STEPS, step, 0)

        def total(self):
            for half in (0, 1):
                for o in range(1, SIDE):
                    s = lax.rem((p.y if half == 0 else p.x) + o, SIDE)
                    ref = parts.at[self.m, half, s]
                    pltpu.make_async_remote_copy(src_ref=ref, dst_ref=ref, send_sem=p_ssem.at[0, 0], recv_sem=p_rsem.at[self.m, half, s],
                                                 device_id={'ep': p.partner}, device_id_type=MESH).wait_recv()
                    pltpu.make_async_copy(ref, part_t.at[half, o - 1], f_sem.at[half, o - 1]).start()
            for half in (0, 1):
                acc = sum_s[self.m, self.STEPS - 2 + half]
                for o in range(1, SIDE):
                    pltpu.make_async_copy(parts.at[self.m, half, 0], part_t.at[half, o - 1], f_sem.at[half, o - 1]).wait()
                    acc = acc + part_t[half, o - 1]
                dx_out[self.m, :, half * wide:(half + 1) * wide] = acc.astype(BF16)

        def finish(self):
            for i in range(self.STEPS - 2):
                self.copy(i).wait_send()

    a, b = gathers
    events = {i: [] for i in range(-1, UNITS)}
    events[-1] += [lambda: a.first(0), lambda: a.first(1), lambda: a.second(0, 0), lambda: a.second(1, 0), b.begin]
    events[0] += [lambda: a.first_far(0), lambda: a.first_far(1)]
    events[1] += [lambda: a.second(0, 1), lambda: a.second(1, 1)]
    events[2] += [lambda: a.second(0, -1), lambda: a.second(1, -1)]
    events[4] += [lambda: a.second(0, 2), lambda: a.second(1, 2)]
    events[5] += [lambda: b.first(0), lambda: b.first(1)]
    events[6] += [lambda: b.second(0, 0), lambda: b.second(1, 0)]
    events[8] += [lambda: a.second_far(0)]
    events[9] += [lambda: b.first_far(0), lambda: b.first_far(1)]
    events[10] += [lambda: a.second_far(1), lambda: a.second_far(-1), lambda: a.second_far(2)]
    events[11] += [lambda: b.second(0, 1), lambda: b.second(1, 1)]
    events[12] += [lambda: b.second(0, -1), lambda: b.second(1, -1)]
    events[14] += [lambda: b.second(0, 2), lambda: b.second(1, 2)]
    for k, (ox, oy) in enumerate(ORDER):
        events[k - 1].append(functools.partial(a.from_partner, ox, oy))
    later = {1: [lambda: b.second_far(0)], 3: [lambda: b.second_far(1), lambda: b.second_far(-1)], 5: [lambda: b.second_far(2)]}

    for e in events[-1]:
        e()
    for g in (g1, g3, g2):
        g[...] = jnp.zeros_like(g)

    def recv_map(k, c):
        s = lax.rem(me + k, group)
        map_copy(s, s, k, s).wait()
        return c

    lax.fori_loop(1, group, recv_map, 0)
    own[0].wait()
    for c in weights:
        c.wait()
    units = (Units(0, ORDER), Units(1, FAR_FIRST))
    sums = (Sums(0), Sums(1))
    units[0].run(events)
    weight_grads(0, later)
    for ox, oy in ORDER:
        b.from_partner(ox, oy)
    own[1].wait()
    units[1].run({})
    for half in (0, 1):
        for o in range(1, SIDE):
            idx_wait(half, o)
    sums[0].run()
    weight_grads(1, {})
    outs = [pltpu.make_async_copy(s, t, g_sem.at[k]) for k, (s, t) in enumerate(((g1, g1_out), (g3, g3_out), (g2, g2_out)))]
    for c in outs:
        c.start()
    sums[1].run()
    for t in sums:
        t.total()

    for g in gathers:
        g.finish()
    for half in (0, 1):
        for o in range(1, SIDE):
            idx_copy(half, o).wait_send()
    for t in units + sums:
        t.finish()
    for c in outs:
        c.wait()


def START(copy):
    copy.start()


def WAIT_SEND(copy):
    copy.wait_send()


def layer_call(group, dy, topk, slots, gates, yd, x, h1, h3, w1, w3, w2):
    n_micro, tokens, d = dy.shape
    f = h1.shape[2]
    top_k = topk.shape[1]
    rows = h1.shape[1] // UNITS
    saved = h1.shape[1]
    hbm = pl.BlockSpec(memory_space=pltpu.HBM)
    vmem = pl.BlockSpec(memory_space=pltpu.VMEM)
    dma = pltpu.SemaphoreType.DMA
    shape = jax.ShapeDtypeStruct
    out = pl.pallas_call(
        functools.partial(layer_kernel, group),
        in_specs=[hbm, vmem, vmem, vmem] + [hbm] * 7,
        out_specs=[vmem, vmem] + [hbm] * 7,
        out_shape=[shape((n_micro, tokens, d), BF16), shape((n_micro, top_k, tokens), F32),
                   shape((d, f), F32), shape((d, f), F32), shape((f, d), F32),
                   shape((n_micro, group, tokens, d), BF16), shape((n_micro, UNITS, rows, d), BF16),
                   shape((n_micro, 2, SIDE, SIDE, rows, d // 2), BF16), shape((n_micro, 2, SIDE, tokens, d // 2), F32)],
        scratch_shapes=[pltpu.VMEM((group, 2 * n_micro, 1, tokens), F32), pltpu.VMEM((group, 2 * n_micro, 1, tokens), F32),
                        pltpu.VMEM((2 * SIDE, n_micro, top_k, tokens), jnp.int32),
                        pltpu.VMEM((d, f), BF16), pltpu.VMEM((d, f), BF16), pltpu.VMEM((f, d), BF16),
                        pltpu.VMEM((2, 2, tokens, d), BF16), pltpu.VMEM((2, rows, f), BF16), pltpu.VMEM((2, rows, f), BF16),
                        pltpu.VMEM((2, rows, d), BF16), pltpu.VMEM((2, 128) + yd.shape[1:], BF16), pltpu.VMEM(dy.shape, BF16),
                        pltpu.VMEM((2, 256, d), BF16), pltpu.VMEM((2, SIDE, rows, d // 2), BF16),
                        pltpu.VMEM((n_micro, 2 * SIDE, tokens, d // 2), F32), pltpu.VMEM((2, SIDE - 1, tokens, d // 2), F32),
                        pltpu.VMEM((saved, d), BF16), pltpu.VMEM((saved, f), BF16), pltpu.VMEM((saved, f), BF16), pltpu.VMEM((saved, f), BF16),
                        pltpu.VMEM((d, f), F32), pltpu.VMEM((d, f), F32), pltpu.VMEM((f, d), F32),
                        dma((n_micro, 80)), dma((n_micro, 80)), dma((group,)), dma((group,)), dma((2 * SIDE,)), dma((2 * SIDE,)),
                        dma((n_micro, 4 * UNITS)), dma((n_micro, 2, SIDE, 2 * SIDE)), dma((n_micro, 2 * SIDE)), dma((n_micro, 2, SIDE)),
                        dma((n_micro + 1,)), dma((3,)), dma((2, 3)), dma((2,)), dma((2,)), dma((2,)), dma((2,)), dma((2, SIDE - 1)), dma((3,))],
        compiler_params=pltpu.CompilerParams(collective_id=0, has_side_effects=True, vmem_limit_bytes=64 * 2**20 - 2**17),
        name='layer')(dy, topk, slots, gates, yd, x, h1, h3, w1, w3, w2)
    return out[:5]


def solution(mesh):
    group = mesh.shape['ep']
    tok_spec = P(None, ('dp', 'ep'))
    w_spec = P('ep')
    grad_w_spec = P(('dp', 'ep'))

    def local_step(grad_out, expert_out, gate_vals, topk_idx, slot_idx, x_dispatch, h1_pre, h3_pre, w_gate, w_up, w_down):
        n_micro, tokens, top_k, d = expert_out.shape
        turned = [jnp.swapaxes(v, 1, 2) for v in (topk_idx, slot_idx, gate_vals)]
        dx, dg, g1, g3, g2 = layer_call(
            group, grad_out, *turned, expert_out.reshape(n_micro * tokens, top_k, d),
            x_dispatch[:, 0], h1_pre[:, 0], h3_pre[:, 0], w_gate[0], w_up[0], w_down[0])
        return dx, jnp.swapaxes(dg, 1, 2), g1[None], g3[None], g2[None]

    in_specs = (tok_spec, tok_spec, tok_spec, tok_spec, tok_spec, tok_spec, tok_spec, tok_spec, w_spec, w_spec, w_spec)
    out_specs = (tok_spec, tok_spec, grad_w_spec, grad_w_spec, grad_w_spec)
    return jax.shard_map(local_step, mesh=mesh, in_specs=in_specs, out_specs=out_specs, check_vma=False)
```

time: 285 us -> 236 us (0.83)
  the two profiles are of different devices: /device:TPU:105 before, /device:TPU:103 now
where the time goes in v3:
time: 236 us; the launch traced here: 233 us
  Pallas kernels  223 us (94%)
  local copies, waits for them, and re-layouts  9.47 us (4%)
    pallas_call x1, Pallas kernels, layer_call(): pl.pallas_call(functools.partial(layer_kernel, group), in_specs=[hbm, vme...  223 us
    unnamed x9, local copies, waits for them, and re-layouts  9.47 us

profile of v3, /device:TPU:103, one launch (start us, length us, event | category | flops | bytes accessed | tf_op | source)
XLA Modules:
  0.0 233.0 jit_solution(13381121872204862601)
XLA Ops:
  0.6 222.9 %layer.1 = (bf16[2,256,1024]{2,1,0:T(8,128)(2,1)}, f32[2,8,256]{2,1,0:T(8,128)}, f32[1024,512]{1,0:T(8,128)}, f32[1024,512]{1,0:T(8,128)}, f32[512,1024]{1,0:T(8...) custom-call(bf16[2,256,1024]{2,1,0:T(8,128)(2,1)} %dy.1, ...), custom_call_target="tpu_custom_call" | custom-call | tf_op jit(solution)/shard_map/layer/pallas_call | solution.py:582
  223.5 0.0 copy-start.1
  223.5 0.0 copy-start
  223.6 2.4 %copy.21 = bf16[2,256,1024]{2,1,0:T(8,128)(2,1)} copy(bf16[2,256,1024]{2,1,0:T(8,128)(2,1)} %get-tuple-element.20) | data formatting | bytes 2097152
  226.0 1.3 copy.22
  227.3 3.1 %copy.23 = f32[1,1024,512]{2,1,0:T(8,128)} copy(f32[1,1024,512]{2,1,0:T(8,128)} %bitcast.20) | data formatting | bytes 4194304
  230.4 0.0 copy-done.1
  230.4 1.3 copy.24
  231.7 0.0 copy-done
  231.7 1.3 copy.25
Async XLA Ops:
  223.5 6.8 %copy-start.1 = (f32[1024,512]{1,0:T(8,128)S(1)}, f32[1024,512]{1,0:T(8,128)}, u32[]{:S(2)}) copy-start(f32[1024,512]{1,0:T(8,128)} %get-tuple-element.13) | copy-start | bytes 6291460
  223.5 8.2 %copy-start = (f32[512,1024]{1,0:T(8,128)S(1)}, f32[512,1024]{1,0:T(8,128)}, u32[]{:S(2)}) copy-start(f32[512,1024]{1,0:T(8,128)} %get-tuple-element.14) | copy-start | bytes 6291460

commit v4 on v3

--- a/solution.py
+++ b/solution.py
@@ -10,9 +10,9 @@
 BF16 = jnp.bfloat16
 MESH = pl.DeviceIdType.MESH
 SIDE = 4
-ORDER = ((0, 0), (1, 0), (3, 0), (0, 1), (0, 3), (1, 1), (3, 3), (1, 3), (3, 1), (2, 0), (0, 2), (2, 1), (1, 2), (2, 3), (3, 2), (2, 2))
+ORDER = [divmod(int(c, 16), SIDE) for c in '04c135f7d8296bea']
 UNITS = len(ORDER)
-FAR_FIRST = ((0, 2), (1, 2), (3, 2), (2, 2), (2, 0), (2, 1), (2, 3), (0, 1), (1, 1), (3, 1), (1, 0), (1, 3), (0, 3), (3, 3), (3, 0), (0, 0))
+FAR_FIRST = [divmod(int(c, 16), SIDE) for c in '26ea89b15d473fc0']
 PART_ORDER = (2, 1, 3, 0)
 
 
@@ -172,11 +172,11 @@
 
 
 def layer_kernel(group, dy, topk, slots, gates, yd, x, h1, h3, w1, w3, w2,
-                 dx_out, dg_out, g1_out, g3_out, g2_out, everyone, staged, lined, parts,
-                 maps, maps_all, idx_all, w1_v, w3_v, w2_v, dy_t, h1_t, h3_t, dx_t, yd_t, dyo, x_t, line_t, sum_s, part_t,
+                 dx_out, dg_out, g1_out, g3_out, g2_out, everyone, staged, lined,
+                 maps, maps_all, idx_all, w1_v, w3_v, w2_v, dy_t, h1_t, h3_t, dx_t, yd_t, dyo, x_t, line_t, sum_s, parts, passing,
                  dyd_s, act_s, dh1_s, dh3_s, g1, g3, g2,
-                 ag_ssem, ag_rsem, m_ssem, m_rsem, i_ssem, i_rsem, r_ssem, r_rsem, p_ssem, p_rsem,
-                 own_sem, w_sem, in_sem, st_sem, yd_sem, x_sem, l_sem, f_sem, g_sem):
+                 ag_ssem, ag_rsem, m_ssem, m_rsem, i_ssem, i_rsem, r_ssem, r_rsem, p_ssem, p_rsem, q_rsem,
+                 own_sem, w_sem, in_sem, st_sem, yd_sem, x_sem, l_sem, g_sem):
     p = Place()
     me = p.me
     n_micro, tokens, d = dy.shape
@@ -438,15 +438,33 @@
             slot = lax.rem(i, 2)
             return pltpu.make_async_copy(lined.at[self.m, half, place], line_t.at[slot], l_sem.at[slot])
 
-        def copy(self, i):
-            half, off, place = self.where(i)
-            chip = jnp.where(half == 0, place * SIDE + p.x, p.y * SIDE + place)
-            mine = jnp.where(half == 0, p.y, p.x)
-            return pltpu.make_async_remote_copy(src_ref=sum_s.at[self.m, i], dst_ref=parts.at[self.m, half, mine], send_sem=p_ssem.at[self.m, i],
-                                                recv_sem=p_rsem.at[self.m, half, mine], device_id={'ep': chip * 2 + p.core}, device_id_type=MESH)
+        def relay(self, i, half, up):
+            home = lax.rem((p.x if half else p.y) + 2, SIDE)
+            step = 1 if up else SIDE - 1
+            to = p.dev(step, 0) if half else p.dev(0, step)
+            return pltpu.make_async_remote_copy(src_ref=sum_s.at[self.m, i, pl.ds(tokens // 2 * up, tokens // 2)], dst_ref=passing.at[self.m, half, up],
+                                                send_sem=p_ssem.at[self.m, i, up], recv_sem=q_rsem.at[self.m, half, up],
+                                                device_id={'ep': to}, device_id_type=MESH)
+
+        def copy(self, i, half, up):
+            step = 1 if up else SIDE - 1
+            to = p.dev(step, 0) if half else p.dev(0, step)
+            return pltpu.make_async_remote_copy(src_ref=sum_s.at[self.m, i], dst_ref=parts.at[self.m, half, up], send_sem=p_ssem.at[self.m, i, 0],
+                                                recv_sem=p_rsem.at[self.m, half, up], device_id={'ep': to}, device_id_type=MESH)
+
+        def sends(self, i):
+            half = i % 2
+            if i < 2:
+                return [self.relay(i, half, up) for up in (0, 1)]
+            if i < self.STEPS - 2:
+                return [self.copy(i, half, 1 - (i // 2 - 1))]
+            return []
+
+        def came(self, ref, sem):
+            pltpu.make_async_remote_copy(src_ref=ref, dst_ref=ref, send_sem=p_ssem.at[0, 0, 0], recv_sem=sem,
+                                         device_id={'ep': p.partner}, device_id_type=MESH).wait_recv()
 
         def run(self):
-            last = self.STEPS - 2
             self.arrive(0)
             self.load(0).start()
 
@@ -457,9 +475,11 @@
                     self.load(i + 1).start()
                 self.load(i).wait()
 
-                @pl.when(jnp.logical_and(i >= 1, i <= last))
-                def _():
-                    self.copy(i - 1).start()
+                for k in range(1, self.STEPS - 1):
+                    @pl.when(i == k)
+                    def _():
+                        for t in self.sends(k - 1):
+                            t.start()
 
                 half, off, place = self.where(i)
                 home = jnp.where(half == 0, place, SIDE + place)
@@ -474,28 +494,30 @@
                     part = dot_tn(jnp.where(hit, 1.0, 0.0).astype(BF16), line_t[slot, s])
                     total = part if total is None else total + part
                 sum_s[self.m, i] = total
+                for k in range(2, self.STEPS - 2):
+                    @pl.when(i == k)
+                    def _():
+                        up = 1 - (k // 2 - 1)
+                        ref = passing.at[self.m, k % 2, up]
+                        self.came(ref, q_rsem.at[self.m, k % 2, up])
+                        cut = pl.ds(tokens // 2 * up, tokens // 2)
+                        sum_s[self.m, k, cut] = sum_s[self.m, k, cut] + passing[self.m, k % 2, up]
                 return c
 
             lax.fori_loop(0, self.STEPS, step, 0)
 
         def total(self):
             for half in (0, 1):
-                for o in range(1, SIDE):
-                    s = lax.rem((p.y if half == 0 else p.x) + o, SIDE)
-                    ref = parts.at[self.m, half, s]
-                    pltpu.make_async_remote_copy(src_ref=ref, dst_ref=ref, send_sem=p_ssem.at[0, 0], recv_sem=p_rsem.at[self.m, half, s],
-                                                 device_id={'ep': p.partner}, device_id_type=MESH).wait_recv()
-                    pltpu.make_async_copy(ref, part_t.at[half, o - 1], f_sem.at[half, o - 1]).start()
-            for half in (0, 1):
                 acc = sum_s[self.m, self.STEPS - 2 + half]
-                for o in range(1, SIDE):
-                    pltpu.make_async_copy(parts.at[self.m, half, 0], part_t.at[half, o - 1], f_sem.at[half, o - 1]).wait()
-                    acc = acc + part_t[half, o - 1]
+                for up in (0, 1):
+                    self.came(parts.at[self.m, half, up], p_rsem.at[self.m, half, up])
+                    acc = acc + parts[self.m, half, up]
                 dx_out[self.m, :, half * wide:(half + 1) * wide] = acc.astype(BF16)
 
         def finish(self):
-            for i in range(self.STEPS - 2):
-                self.copy(i).wait_send()
+            for i in range(self.STEPS):
+                for t in self.sends(i):
+                    t.wait_send()
 
     a, b = gathers
     events = {i: [] for i in range(-1, UNITS)}
@@ -582,26 +604,57 @@
     out = pl.pallas_call(
         functools.partial(layer_kernel, group),
         in_specs=[hbm, vmem, vmem, vmem] + [hbm] * 7,
-        out_specs=[vmem, vmem] + [hbm] * 7,
+        out_specs=[vmem, vmem] + [hbm] * 6,
         out_shape=[shape((n_micro, tokens, d), BF16), shape((n_micro, top_k, tokens), F32),
                    shape((d, f), F32), shape((d, f), F32), shape((f, d), F32),
                    shape((n_micro, group, tokens, d), BF16), shape((n_micro, UNITS, rows, d), BF16),
-                   shape((n_micro, 2, SIDE, SIDE, rows, d // 2), BF16), shape((n_micro, 2, SIDE, tokens, d // 2), F32)],
+                   shape((n_micro, 2, SIDE, SIDE, rows, d // 2), BF16)],
         scratch_shapes=[pltpu.VMEM((group, 2 * n_micro, 1, tokens), F32), pltpu.VMEM((group, 2 * n_micro, 1, tokens), F32),
                         pltpu.VMEM((2 * SIDE, n_micro, top_k, tokens), jnp.int32),
                         pltpu.VMEM((d, f), BF16), pltpu.VMEM((d, f), BF16), pltpu.VMEM((f, d), BF16),
                         pltpu.VMEM((2, 2, tokens, d), BF16), pltpu.VMEM((2, rows, f), BF16), pltpu.VMEM((2, rows, f), BF16),
                         pltpu.VMEM((2, rows, d), BF16), pltpu.VMEM((2, 128) + yd.shape[1:], BF16), pltpu.VMEM(dy.shape, BF16),
                         pltpu.VMEM((2, 256, d), BF16), pltpu.VMEM((2, SIDE, rows, d // 2), BF16),
-                        pltpu.VMEM((n_micro, 2 * SIDE, tokens, d // 2), F32), pltpu.VMEM((2, SIDE - 1, tokens, d // 2), F32),
+                        pltpu.VMEM((n_micro, 2 * SIDE, tokens, d // 2), F32), pltpu.VMEM((n_micro, 2, 2, tokens, d // 2), F32), pltpu.VMEM((n_micro, 2, 2, tokens // 2, d // 2), F32),
                         pltpu.VMEM((saved, d), BF16), pltpu.VMEM((saved, f), BF16), pltpu.VMEM((saved, f), BF16), pltpu.VMEM((saved, f), BF16),
                         pltpu.VMEM((d, f), F32), pltpu.VMEM((d, f), F32), pltpu.VMEM((f, d), F32),
                         dma((n_micro, 80)), dma((n_micro, 80)), dma((group,)), dma((group,)), dma((2 * SIDE,)), dma((2 * SIDE,)),
-                        dma((n_micro, 4 * UNITS)), dma((n_micro, 2, SIDE, 2 * SIDE)), dma((n_micro, 2 * SIDE)), dma((n_micro, 2, SIDE)),
-                        dma((n_micro + 1,)), dma((3,)), dma((2, 3)), dma((2,)), dma((2,)), dma((2,)), dma((2,)), dma((2, SIDE - 1)), dma((3,))],
+                        dma((n_micro, 4 * UNITS)), dma((n_micro, 2, SIDE, 2 * SIDE)), dma((n_micro, 2 * SIDE, 2)), dma((n_micro, 2, 2)), dma((n_micro, 2, 2)),
+                        dma((n_micro + 1,)), dma((3,)), dma((2, 3)), dma((2,)), dma((2,)), dma((2,)), dma((2,)), dma((3,))],
         compiler_params=pltpu.CompilerParams(collective_id=0, has_side_effects=True, vmem_limit_bytes=64 * 2**20 - 2**17),
         name='layer')(dy, topk, slots, gates, yd, x, h1, h3, w1, w3, w2)
     return out[:5]
+
+
+def pass_on_kernel(n, cuts, *refs):
+    src, dst, held, (sem_in, sem_out) = refs[:n], refs[n:2 * n], refs[2 * n:3 * n], refs[3 * n:]
+    jobs = []
+    for a in range(n):
+        size = src[a].shape[0] // cuts[a]
+        for k in range(cuts[a]):
+            at = pl.ds(k * size, size)
+            jobs.append((src[a].at[at], held[a].at[at], dst[a].at[at]))
+    moves = [(pltpu.make_async_copy(s, h, sem_in.at[k]), pltpu.make_async_copy(h, t, sem_out.at[k])) for k, (s, h, t) in enumerate(jobs)]
+    for load, store in moves:
+        load.start()
+    for load, store in moves:
+        load.wait()
+        store.start()
+    for load, store in moves:
+        store.wait()
+
+
+def pass_on(values, cuts):
+    hbm = pl.BlockSpec(memory_space=pltpu.HBM)
+    n = len(values)
+    jobs = sum(cuts)
+    return pl.pallas_call(
+        functools.partial(pass_on_kernel, n, cuts),
+        in_specs=[hbm] * n, out_specs=[hbm] * n,
+        out_shape=[jax.ShapeDtypeStruct(v.shape, v.dtype) for v in values],
+        scratch_shapes=[pltpu.VMEM(v.shape, v.dtype) for v in values] + [pltpu.SemaphoreType.DMA((jobs,)), pltpu.SemaphoreType.DMA((jobs,))],
+        compiler_params=pltpu.CompilerParams(vmem_limit_bytes=64 * 2**20 - 2**17),
+        name='pass_on')(*values)
 
 
 def solution(mesh):
@@ -616,6 +669,7 @@
         dx, dg, g1, g3, g2 = layer_call(
             group, grad_out, *turned, expert_out.reshape(n_micro * tokens, top_k, d),
             x_dispatch[:, 0], h1_pre[:, 0], h3_pre[:, 0], w_gate[0], w_up[0], w_down[0])
+        dx, dg, g1, g3, g2 = pass_on((dx, dg, g1, g3, g2), (n_micro, 1, 4, 4, 4))
         return dx, jnp.swapaxes(dg, 1, 2), g1[None], g3[None], g2[None]
 
     in_specs = (tok_spec, tok_spec, tok_spec, tok_spec, tok_spec, tok_spec, tok_spec, tok_spec, w_spec, w_spec, w_spec)

time: 236 us -> 231 us (0.979)
  local copies, waits for them, and re-layouts: 9.47 us -> 0 us
  Pallas kernels: 223 us -> 226 us
    unnamed x9 -> x0, local copies, waits for them, and re-layouts: 9.47 us -> none
    pallas_call x0 -> x1, Pallas kernels: none -> 6 us  [pass_on(): pl.pallas_call(functools.partial(pass_on_kernel, n, cuts), in_specs=[hbm]...]
    pallas_call x1, Pallas kernels: 223 us -> 220 us  [layer_call(): pl.pallas_call(functools.partial(layer_kernel, group), in_specs=[hbm, vme...]
where the time goes in v4:
time: 231 us; the launch traced here: 227 us
  Pallas kernels  226 us (98%)
    pallas_call x1, Pallas kernels, layer_call(): pl.pallas_call(functools.partial(layer_kernel, group), in_specs=[hbm, vme...  220 us
    pallas_call x1, Pallas kernels, pass_on(): pl.pallas_call(functools.partial(pass_on_kernel, n, cuts), in_specs=[hbm]...  6 us

profile of v4, /device:TPU:103, one launch (start us, length us, event | category | flops | bytes accessed | tf_op | source)
XLA Modules:
  0.0 227.0 jit_solution(5827609375537530141)
XLA Ops:
  0.6 220.2 %layer.1 = (bf16[2,256,1024]{2,1,0:T(8,128)(2,1)}, f32[2,8,256]{2,1,0:T(8,128)}, f32[1024,512]{1,0:T(8,128)}, f32[1024,512]{1,0:T(8,128)}, f32[512,1024]{1,0:T(8...) custom-call(bf16[2,256,1024]{2,1,0:T(8,128)(2,1)} %dy.1, ...), custom_call_target="tpu_custom_call" | custom-call | tf_op jit(solution)/shard_map/layer/pallas_call | solution.py:604
  220.9 6.0 %pass_on.1 = (bf16[2,256,1024]{2,1,0:T(8,128)(2,1)}, f32[2,8,256]{2,1,0:T(8,128)}, f32[1024,512]{1,0:T(8,128)}, f32[1024,512]{1,0:T(8,128)}, f32[512,1024]{1,0:T(8,128)}) custom-call(bf16[2,256,1024]{2,1,0:T(8,128)(2,1)} %get-tuple-element.15.refs_0_, f32[2,8,256]{2,1,0:T(8,128)} %get-tuple-element.16.refs_1_, f32[1024,512]{1,0:T(8,128)} %get-tuple-element.17.refs_2_, ...), custom_call_target="tpu_custom_call" | custom-call | tf_op jit(solution)/shard_map/pass_on/pallas_call | solution.py:651

commit v5 on v4

--- a/solution.py
+++ b/solution.py
@@ -564,11 +564,11 @@
         for o in range(1, SIDE):
             idx_wait(half, o)
     sums[0].run()
+    sums[1].run()
     weight_grads(1, {})
     outs = [pltpu.make_async_copy(s, t, g_sem.at[k]) for k, (s, t) in enumerate(((g1, g1_out), (g3, g3_out), (g2, g2_out)))]
     for c in outs:
         c.start()
-    sums[1].run()
     for t in sums:
         t.total()
 

time: 231 us -> 226 us (0.978)
  Pallas kernels: 226 us -> 221 us
    pallas_call x1, Pallas kernels: 220 us -> 215 us  [layer_call(): pl.pallas_call(functools.partial(layer_kernel, group), in_specs=[hbm, vme...]
where the time goes in v5:
time: 226 us; the launch traced here: 221 us
  Pallas kernels  221 us (98%)
    pallas_call x1, Pallas kernels, layer_call(): pl.pallas_call(functools.partial(layer_kernel, group), in_specs=[hbm, vme...  215 us
    pallas_call x1, Pallas kernels, pass_on(): pl.pallas_call(functools.partial(pass_on_kernel, n, cuts), in_specs=[hbm]...  6 us

profile of v5, /device:TPU:103, one launch (start us, length us, event | category | flops | bytes accessed | tf_op | source)
XLA Modules:
  0.0 221.5 jit_solution(5565618158112814888)
XLA Ops:
  0.6 214.7 %layer.1 = (bf16[2,256,1024]{2,1,0:T(8,128)(2,1)}, f32[2,8,256]{2,1,0:T(8,128)}, f32[1024,512]{1,0:T(8,128)}, f32[1024,512]{1,0:T(8,128)}, f32[512,1024]{1,0:T(8...) custom-call(bf16[2,256,1024]{2,1,0:T(8,128)(2,1)} %dy.1, ...), custom_call_target="tpu_custom_call" | custom-call | tf_op jit(solution)/shard_map/layer/pallas_call | solution.py:604
  215.3 6.0 %pass_on.1 = (bf16[2,256,1024]{2,1,0:T(8,128)(2,1)}, f32[2,8,256]{2,1,0:T(8,128)}, f32[1024,512]{1,0:T(8,128)}, f32[1024,512]{1,0:T(8,128)}, f32[512,1024]{1,0:T(8,128)}) custom-call(bf16[2,256,1024]{2,1,0:T(8,128)(2,1)} %get-tuple-element.15.refs_0_, f32[2,8,256]{2,1,0:T(8,128)} %get-tuple-element.16.refs_1_, f32[1024,512]{1,0:T(8,128)} %get-tuple-element.17.refs_2_, ...), custom_call_target="tpu_custom_call" | custom-call | tf_op jit(solution)/shard_map/pass_on/pallas_call | solution.py:651
